TPU v7x, 128 devices: a whole 4x4x4 slice. The times are simulated.
128 devices in a mesh: model: 64 (over z, y, x), fsdp: 2 (over core).
Axes of the slice: x: 4, y: 4, z: 4, core: 2. Of those that a mesh axis runs over, the one named last changes fastest.
Arguments:
- tok_ids: int32 [2, 1024], P('fsdp')
- tok_labels: int32 [2, 1024], P('fsdp')
- emb_table: bfloat16 [50304, 1024], P(('model', 'fsdp'))
- w_gate: bfloat16 [1024, 4096], P('fsdp')
- w_up: bfloat16 [1024, 4096], P('fsdp')
- w_down: bfloat16 [4096, 1024], P('fsdp')
- gain_in: float32 [1024], replicated
- gain_out: float32 [1024], replicated
Outputs:
- output 1: float32 [], replicated
- output 2: float32 [50304, 1024], P(('model', 'fsdp'))
- output 3: float32 [1024, 4096], P('fsdp')
- output 4: float32 [1024, 4096], P('fsdp')
- output 5: float32 [4096, 1024], P('fsdp')
All inputs are finite; a program needn't handle non-finite values.
Results may differ from a plain program's by a relative error of at most 0.0118123.
Values are sent between devices in bfloat16 or wider.
A program may use at most 1 GiB of HBM per device.

v0:
```python
import jax
import jax.numpy as jnp
from jax import lax
from jax.sharding import PartitionSpec as P

EPS = 1e-6


def rms_scale(values, gain_vec):
    mean_sq = jnp.mean(values * values, axis=-1, keepdims=True)
    return values * lax.rsqrt(mean_sq + EPS) * gain_vec


def mlp_forward(x_emb, gain_in, w_gate, w_up, w_down):
    normed_in, norm_in_back = jax.vjp(lambda values: rms_scale(values, gain_in), x_emb)
    normed_bf = normed_in.astype(jnp.bfloat16)
    gate_f = jnp.dot(normed_bf, w_gate, preferred_element_type=jnp.float32).astype(jnp.bfloat16).astype(jnp.float32)
    up_f = jnp.dot(normed_bf, w_up, preferred_element_type=jnp.float32).astype(jnp.bfloat16).astype(jnp.float32)
    gate_sig = jax.nn.sigmoid(gate_f)
    silu_gate = gate_f * gate_sig
    act_bf = (silu_gate * up_f).astype(jnp.bfloat16)
    mlp_out = jnp.dot(act_bf, w_down, preferred_element_type=jnp.float32).astype(jnp.bfloat16)
    h_res = x_emb + mlp_out.astype(jnp.float32)
    return h_res, (norm_in_back, normed_bf, gate_f, up_f, gate_sig, silu_gate, act_bf)


def mlp_backward(d_hidden, saved, w_gate, w_up, w_down):
    norm_in_back, normed_bf, gate_f, up_f, gate_sig, silu_gate, act_bf = saved
    d_mlp = d_hidden.astype(jnp.bfloat16)
    d_act = jnp.einsum("td,fd->tf", d_mlp, w_down, preferred_element_type=jnp.float32)
    grad_down = jnp.einsum("tf,td->fd", act_bf, d_mlp, preferred_element_type=jnp.float32)
    d_gate = (d_act * up_f * (gate_sig * (1.0 + gate_f * (1.0 - gate_sig)))).astype(jnp.bfloat16)
    d_up = (d_act * silu_gate).astype(jnp.bfloat16)
    grad_gate = jnp.einsum("td,tf->df", normed_bf, d_gate, preferred_element_type=jnp.float32)
    grad_up = jnp.einsum("td,tf->df", normed_bf, d_up, preferred_element_type=jnp.float32)
    d_normed = jnp.einsum("tf,df->td", d_gate, w_gate, preferred_element_type=jnp.float32) + jnp.einsum("tf,df->td", d_up, w_up, preferred_element_type=jnp.float32)
    d_x = d_hidden + norm_in_back(d_normed)[0]
    return d_x, grad_gate, grad_up, grad_down


def solution(mesh):
    fsdp_size = mesh.shape["fsdp"]
    tok_spec = P("fsdp", None)
    row_spec = P(("model", "fsdp"), None)
    weight_spec = P("fsdp", None)

    def device_step(tok_ids, tok_labels, table_shard, gate_shard, up_shard, down_shard, gain_in, gain_out):
        local_count = tok_ids.shape[0] * tok_ids.shape[1]
        num_tokens = local_count * fsdp_size
        table_part = lax.all_gather(table_shard, "fsdp", axis=0, tiled=True)
        w_gate = lax.all_gather(gate_shard, "fsdp", axis=0, tiled=True)
        w_up = lax.all_gather(up_shard, "fsdp", axis=0, tiled=True)
        w_down = lax.all_gather(down_shard, "fsdp", axis=0, tiled=True)
        vocab_part = table_part.shape[0]
        vocab_start = lax.axis_index("model") * vocab_part
        local_ids = tok_ids.reshape(local_count) - vocab_start
        id_inside = (local_ids >= 0) & (local_ids < vocab_part)
        safe_ids = jnp.where(id_inside, local_ids, 0)
        emb_rows = jnp.where(id_inside[:, None], jnp.take(table_part, safe_ids, axis=0), 0)
        x_emb = lax.psum(emb_rows, "model").astype(jnp.float32)
        h_res, saved = mlp_forward(x_emb, gain_in, w_gate, w_up, w_down)
        hn_f, norm_out_back = jax.vjp(lambda values: rms_scale(values, gain_out), h_res)
        hn_bf = hn_f.astype(jnp.bfloat16)
        logits = jnp.einsum("td,vd->tv", hn_bf, table_part, preferred_element_type=jnp.float32)
        row_max = lax.pmax(jnp.max(logits, axis=-1), "model")
        exp_shift = jnp.exp(logits - row_max[:, None])
        local_labels = tok_labels.reshape(local_count) - vocab_start
        onehot = lax.broadcasted_iota(jnp.int32, logits.shape, 1) == local_labels[:, None]
        part_stats = jnp.stack([jnp.sum(exp_shift, axis=-1), jnp.sum(jnp.where(onehot, logits, 0.0), axis=-1)])
        tok_stats = lax.psum(part_stats, "model")
        sum_exp = tok_stats[0]
        tok_loss = row_max + jnp.log(sum_exp) - tok_stats[1]
        loss = lax.psum(jnp.sum(tok_loss), "fsdp") / num_tokens
        soft_probs = exp_shift / sum_exp[:, None]
        d_logits = (jnp.where(onehot, soft_probs - 1.0, soft_probs) / num_tokens).astype(jnp.bfloat16)
        d_head = jnp.einsum("tv,td->vd", d_logits, hn_bf, preferred_element_type=jnp.float32)
        d_hn = lax.psum(jnp.einsum("tv,vd->td", d_logits, table_part, preferred_element_type=jnp.float32), "model")
        d_hidden = norm_out_back(d_hn)[0]
        d_x, grad_gate, grad_up, grad_down = mlp_backward(d_hidden, saved, w_gate, w_up, w_down)
        d_in = jax.ops.segment_sum(jnp.where(id_inside[:, None], d_x, 0.0), safe_ids, num_segments=vocab_part)
        grad_table = lax.psum_scatter(d_head + d_in, "fsdp", scatter_dimension=0, tiled=True)
        grad_gate = lax.psum_scatter(grad_gate, "fsdp", scatter_dimension=0, tiled=True)
        grad_up = lax.psum_scatter(grad_up, "fsdp", scatter_dimension=0, tiled=True)
        grad_down = lax.psum_scatter(grad_down, "fsdp", scatter_dimension=0, tiled=True)
        return loss, grad_table, grad_gate, grad_up, grad_down

    return jax.shard_map(device_step, mesh=mesh, in_specs=(tok_spec, tok_spec, row_spec, weight_spec, weight_spec, weight_spec, P(), P()), out_specs=(P(), row_spec, weight_spec, weight_spec, weight_spec), check_vma=False)
```

profile of v0, /device:TPU:1, one launch (start us, length us, event | category | flops | bytes accessed | tf_op | source)
XLA Modules:
  0.0 936.4 jit_solution(3375012372630988834)
XLA Ops:
  7.2 0.0 all-gather.12.cloned.1.call-start
  7.2 0.7 all-gather.12.cloned.1.call-update
  7.9 0.0 all-reduce.5.cloned.1.call-start
  8.0 1.3 compare_select_fusion
  9.3 16.6 %all-gather.12.cloned.1.call-done = bf16[2,393,1024]{2,1,0:T(8,128)(2,1)} async-done(((bf16[1,393,1024]{2,1,0:T(8,128)(2,1)}), bf16[2,393,1024]{2,1,0:T(8,128)(2,1)}) %all-gather.12.cloned.1.call-update) | async-done | bytes 1609744 | tf_op jit(solution)/shard_map/all_gather | solution.py:50
  25.9 1.7 reshape.120
  27.6 5.3 gather_fusion
  32.9 3.9 copy.18
  36.9 3.1 select_select_fusion
  40.0 0.0 all-reduce.5.cloned.1.call-update
  40.0 0.0 all-gather.8.cloned.1.call-start
  40.1 0.7 all-gather.8.cloned.1.call-update
  40.8 0.0 copy-start.17
  40.8 0.0 all-gather.6.cloned.1.call-start
  40.8 0.5 all-gather.6.cloned.1.call-update
  41.4 0.0 copy-start.19
  41.4 0.0 all-gather.10.cloned.1.call-start
  41.4 0.5 all-gather.10.cloned.1.call-update
  42.0 0.0 all-reduce.7.cloned.1.call-start
  42.1 130.7 %all-reduce.5.cloned.1.call-done = bf16[1024,1024]{0,1:T(8,128)(2,1)} async-done(((bf16[1024,1024]{0,1:T(8,128)(2,1)}), bf16[1024,1024]{0,1:T(8,128)(2,1)}) %all-reduce.5.cloned.1.call-update) | async-done | bytes 2097168 | tf_op jit(solution)/shard_map/psum | solution.py:60
  172.7 2.1 fusion.11
  174.8 0.6 copy-done.6
  175.4 22.3 %all-gather.8.cloned.1.call-done = bf16[1024,4096]{1,0:T(8,128)(2,1)} async-done(((bf16[512,4096]{1,0:T(8,128)(2,1)}), bf16[1024,4096]{1,0:T(8,128)(2,1)}) %all-gather.8.cloned.1.call-update) | async-done | bytes 8388624 | tf_op jit(solution)/shard_map/all_gather | solution.py:52
  197.7 15.2 %convolution_convert_fusion = bf16[1024,4096]{1,0:T(8,128)(2,1)} fusion(bf16[1024,4096]{1,0:T(8,128)(2,1)} %all-gather.8.cloned.1.call-done, bf16[1024,1024]{0,1:T(8,128)(2,1)} %all-reduce.5.cloned.1.call-done, f32[1024]{0:T(1024)S(1)} %copy-done.19, f32[1024]{0:T(1024)S(1)} %fusion.22), kind=kOutput, calls=%fused_computation.21 | convolution fusion | flops 8598323200 | bytes 18882560 | tf_op jit(solution)/shard_map/dot_general | solution.py:18
  212.9 11.2 %all-gather.6.cloned.1.call-done = bf16[1024,4096]{1,0:T(8,128)(2,1)} async-done(((bf16[512,4096]{1,0:T(8,128)(2,1)}), bf16[1024,4096]{1,0:T(8,128)(2,1)}) %all-gather.6.cloned.1.call-update) | async-done | bytes 8388624 | tf_op jit(solution)/shard_map/all_gather | solution.py:51
  224.1 15.2 %convolution_convert_fusion.1 = bf16[1024,4096]{1,0:T(8,128)(2,1)} fusion(bf16[1024,4096]{1,0:T(8,128)(2,1)} %all-gather.6.cloned.1.call-done, bf16[1024,1024]{0,1:T(8,128)(2,1)} %all-reduce.5.cloned.1.call-done, f32[1024]{0:T(1024)S(1)} %copy-done.19, f32[1024]{0:T(1024)S(1)} %fusion.22), kind=kOutput, calls=%fused_computation.22 | convolution fusion | flops 8598323200 | bytes 18882560 | tf_op jit(solution)/shard_map/dot_general | solution.py:17
  239.3 11.2 %all-gather.10.cloned.1.call-done = bf16[4096,1024]{1,0:T(8,128)(2,1)} async-done(((bf16[2048,1024]{1,0:T(8,128)(2,1)}), bf16[4096,1024]{1,0:T(8,128)(2,1)}) %all-gather.10.cloned.1.call-update) | async-done | bytes 8388624 | tf_op jit(solution)/shard_map/all_gather | solution.py:53
  250.5 18.5 %multiply_reduce_fusion.1 = (f32[1024]{0:T(1024)S(1)}, bf16[1024,1024]{0,1:T(8,128)(2,1)}) fusion(bf16[1024,1024]{0,1:T(8,128)(2,1)} %all-reduce.5.cloned.1.call-done, bf16[4096,1024]{1,0:T(8,128)(2,1)} %all-gather.10.cloned.1.call-done, bf16[1024,4096]{1,0:T(8,128)(2,1)} %convolution_convert_fusion, bf16[1024,4096]{1,0:T(8,128)(2,1)} %convolution_convert_fusion.1), kind=kOutput, calls=%fused_computation.35 | convolution fusion | flops 8629779456 | bytes 29364224 | tf_op jit(solution)/shard_map/dot_general | solution.py:22
  268.9 6.0 fusion.35
  275.0 150.9 %pmax.7 = f32[1024]{0:T(1024)S(1)} all-reduce(f32[1024]{0:T(1024)S(1)} %get-tuple-element.18), channel_id=1, replica_groups=mesh['model'=64,'fsdp'=2] {'model'}, use_global_device_ids=true, to_apply=%region_4.5 | all-reduce | flops 1024 | bytes 8192 | tf_op jit(solution)/shard_map/pmax | solution.py:65
  425.9 2.8 fusion.17
  428.7 145.9 %psum.29 = f32[2,1024]{1,0:T(2,128)S(1)} all-reduce(f32[2,1024]{1,0:T(2,128)S(1)} %pad_maximum_fusion), channel_id=1, replica_groups=mesh['model'=64,'fsdp'=2] {'model'}, use_global_device_ids=true, to_apply=%region_7.8 | all-reduce | flops 2048 | bytes 16384 | tf_op jit(solution)/shard_map/psum | solution.py:70
  574.7 0.6 fusion.34
  575.3 0.6 copy-done.11
  575.9 6.4 fusion.36
  582.3 0.0 all-reduce.7.cloned.1.call-update
  582.3 0.0 reduce-scatter.6.cloned.1.call-start
  582.4 189.0 %all-reduce.7.cloned.1.call-done = f32[1024,1024]{0,1:T(8,128)} async-done(((f32[1024,1024]{0,1:T(8,128)}), f32[1024,1024]{0,1:T(8,128)}) %all-reduce.7.cloned.1.call-update) | async-done | bytes 4194320 | tf_op jit(solution)/shard_map/psum | solution.py:77
  771.4 3.7 multiply_reduce_fusion
  775.1 25.4 %multiply_convert_fusion = (bf16[1024,4096]{1,0:T(8,128)(2,1)}, bf16[1024,4096]{1,0:T(8,128)(2,1)}) fusion(bf16[1024,4096]{1,0:T(8,128)(2,1)} %convolution_convert_fusion.1, bf16[1024,4096]{1,0:T(8,128)(2,1)} %convolution_convert_fusion, bf16[4096,1024]{1,0:T(8,128)(2,1)} %all-gather.10.cloned.1.call-done, f32[1024]{0:T(1024)S(1)} %multiply_multiply_fusion.1, ...), kind=kOutput, calls=%fused_computation.15 | convolution fusion | flops 8662286336 | bytes 50343936 | tf_op jit(solution)/shard_map/td,fd->tf/dot_general | solution.py:30
  800.6 14.6 %fusion.28 = f32[1024,4096]{1,0:T(8,128)} fusion(bf16[1024,4096]{1,0:T(8,128)(2,1)} %get-tuple-element.11, bf16[1024,1024]{0,1:T(8,128)(2,1)S(1)} %copy-done, f32[1024]{0:T(1024)S(1)} %copy-done.19, f32[1024]{0:T(1024)S(1)} %fusion.22), kind=kOutput, calls=%fused_computation.68 | convolution fusion | flops 8594128896 | bytes 27271168 | tf_op jit(solution)/shard_map/td,tf->df/dot_general | solution.py:34
  815.1 0.0 reduce-scatter.6.cloned.1.call-update
  815.1 0.0 reduce-scatter.8.cloned.1.call-start
  815.2 14.6 %fusion.26 = f32[1024,4096]{1,0:T(8,128)} fusion(bf16[1024,4096]{1,0:T(8,128)(2,1)} %get-tuple-element.10, bf16[1024,1024]{0,1:T(8,128)(2,1)S(1)} %copy-done, f32[1024]{0:T(1024)S(1)} %copy-done.19, f32[1024]{0:T(1024)S(1)} %fusion.22), kind=kOutput, calls=%fused_computation.67 | convolution fusion | flops 8594128896 | bytes 27271168 | tf_op jit(solution)/shard_map/td,tf->df/dot_general | solution.py:35
  829.8 0.0 reduce-scatter.8.cloned.1.call-update
  829.8 0.0 reduce-scatter.10.cloned.1.call-start
  829.9 21.0 %fusion.18 = f32[4096,1024]{1,0:T(8,128)} fusion(f32[1024,1024]{0,1:T(8,128)} %all-reduce.7.cloned.1.call-done, bf16[1024,1024]{0,1:T(8,128)(2,1)} %get-tuple-element.17, bf16[1024,1024]{0,1:T(8,128)(2,1)S(1)} %copy-done, f32[1024]{0:T(1024)S(1)} %multiply_multiply_fusion.1, f32[1024]{0:T(1024)S(1)} %copy-done.14, f32[1024]{0:T(1024)S(1)} %fusion.23, ...), kind=kOutput, calls=%fused_computation.44 | convolution fusion | flops 8632926208 | bytes 41955328 | tf_op jit(solution)/shard_map/tf,td->fd/dot_general | solution.py:31
  850.9 0.0 reduce-scatter.10.cloned.1.call-update
  850.9 0.6 copy-done.18
  851.5 0.6 dynamic-slice.4
  852.8 5.7 fusion.24
  858.5 13.1 %fusion.39 = f32[1024,1024]{0,1:T(8,128)S(1)} fusion(bf16[1024,4096]{1,0:T(8,128)(2,1)} %get-tuple-element.11, bf16[1024,4096]{1,0:T(8,128)(2,1)} %all-gather.6.cloned.1.call-done), kind=kOutput, calls=%fused_computation.72 | convolution fusion | flops 8589934592 | bytes 20971520 | tf_op jit(solution)/shard_map/tf,df->td/dot_general | solution.py:36
  871.6 14.2 %fusion.14 = (f32[1024]{0:T(1024)S(1)}, f32[1024,1024]{0,1:T(8,128)S(1)}) fusion(bf16[1024,1024]{0,1:T(8,128)(2,1)S(1)} %copy-done.1, f32[1024]{0:T(1024)S(1)} %copy-done.19, f32[1024,1024]{0,1:T(8,128)S(1)} %fusion.39, bf16[1024,4096]{1,0:T(8,128)(2,1)} %get-tuple-element.10, bf16[1024,4096]{1,0:T(8,128)(2,1)} %all-gather.8.cloned.1.call-done), kind=kOutput, calls=%fused_computation.31 | convolution fusion | flops 8595176448 | bytes 27271168 | tf_op jit(solution)/shard_map/tf,df->td/dot_general | solution.py:36
  885.9 3.9 fusion.10
  889.8 5.4 copy.20
  895.2 11.5 %scatter_fusion = f32[786,1024]{1,0:T(8,128)S(1)} fusion(f32[786,1024]{1,0:T(8,128)S(1)} %fusion.24, s32[1024]{0:T(1024)S(1)} %bitcast.31, f32[1024,1024]{1,0:T(8,128)} %copy.20), kind=kCustom, calls=%fused_computation.1 | custom fusion | flops 1048576 | bytes 12587008 | tf_op jit(solution)/shard_map/scatter-add | solution.py:80
  906.7 8.5 fusion
  915.2 0.8 slice.12
  916.0 1.3 collective-permute-start
  917.2 0.6 subtract_reduce_fusion
  917.9 3.9 psum.30
  922.4 0.0 collective-permute-done
  922.4 4.5 concatenate
  926.9 1.4 constant_dynamic-slice_fusion
  (46 shorter events, 0.1 us)
Async XLA Ops:
  7.2 18.7 %all-gather.12.cloned.1.call-start = ((), (), s32[]{:S(2)}) async-start(), calls=%async_computation.11 | async-start | bytes 2457600 | tf_op jit(solution)/shard_map/all_gather | solution.py:50
  7.9 164.8 %all-reduce.5.cloned.1.call-start = ((), (), s32[]{:S(2)}) async-start(), calls=%async_computation.3 | async-start | bytes 4194304 | tf_op jit(solution)/shard_map/psum | solution.py:60
  9.3 27.6 %copy-start.15 = (pred[1024]{0:T(1024)(128)(4,1)}, pred[1024]{0:T(1024)(128)(4,1)S(1)}, u32[]{:S(2)}) copy-start(pred[1024]{0:T(1024)(128)(4,1)S(1)} %get-tuple-element.14) | copy-start | bytes 3076
  40.0 157.7 %all-gather.8.cloned.1.call-start = ((), (), s32[]{:S(2)}) async-start(), calls=%async_computation.5 | async-start | bytes 12582912 | tf_op jit(solution)/shard_map/all_gather | solution.py:52
  40.8 1.2 copy-start.17
  40.8 183.3 %all-gather.6.cloned.1.call-start = ((), (), s32[]{:S(2)}) async-start(), calls=%async_computation.4 | async-start | bytes 12582912 | tf_op jit(solution)/shard_map/all_gather | solution.py:51
  41.4 156.3 %copy-start.19 = (f32[1024]{0:T(1024)S(1)}, f32[1024]{0:T(1024)}, u32[]{:S(2)}) copy-start(f32[1024]{0:T(1024)} %param.14) | copy-start | bytes 12292
  41.4 209.1 %all-gather.10.cloned.1.call-start = ((), (), s32[]{:S(2)}) async-start(), calls=%async_computation.6 | async-start | bytes 12582912 | tf_op jit(solution)/shard_map/all_gather | solution.py:53
  42.0 729.4 %all-reduce.7.cloned.1.call-start = ((), (), s32[]{:S(2)}) async-start(), calls=%async_computation.7 | async-start | bytes 8388608 | tf_op jit(solution)/shard_map/psum | solution.py:77
  42.0 533.2 %copy-start.8 = (s32[1,1024]{1,0:T(1,128)}, s32[1,1024]{1,0:T(1,128)S(1)}, u32[]{:S(2)}) copy-start(s32[1,1024]{1,0:T(1,128)S(1)} %broadcast_subtract_fusion) | copy-start | bytes 12292
  174.8 0.6 copy-start.6
  239.3 29.7 %copy-start.14 = (f32[1024]{0:T(1024)S(1)}, f32[1024]{0:T(1024)}, u32[]{:S(2)}) copy-start(f32[1024]{0:T(1024)} %param.15) | copy-start | bytes 12292
  425.9 149.4 %copy-start.4 = (f32[1024]{0:T(1024)}, f32[1024]{0:T(1024)S(1)}, u32[]{:S(2)}) copy-start(f32[1024]{0:T(1024)S(1)} %pmax.7) | copy-start | bytes 12292
  575.3 0.6 copy-start.11
  582.3 189.1 %copy-start = (bf16[1024,1024]{0,1:T(8,128)(2,1)S(1)}, bf16[1024,1024]{0,1:T(8,128)(2,1)}, u32[]{:S(2)}) copy-start(bf16[1024,1024]{0,1:T(8,128)(2,1)} %all-reduce.5.cloned.1.call-done) | copy-start | bytes 6291460
  582.3 345.9 %reduce-scatter.6.cloned.1.call-start = ((), (), s32[]{:S(2)}) async-start(), calls=%async_computation.8 | async-start | bytes 25165824 | tf_op jit(solution)/shard_map/reduce_scatter | solution.py:82
  815.1 113.1 %reduce-scatter.8.cloned.1.call-start = ((), (), s32[]{:S(2)}) async-start(), calls=%async_computation.9 | async-start | bytes 25165824 | tf_op jit(solution)/shard_map/reduce_scatter | solution.py:83
  829.8 98.5 %reduce-scatter.10.cloned.1.call-start = ((), (), s32[]{:S(2)}) async-start(), calls=%async_computation.10 | async-start | bytes 25165824 | tf_op jit(solution)/shard_map/reduce_scatter | solution.py:84
  850.9 0.7 copy-start.18
  850.9 1.9 copy-start.5
  850.9 1.9 copy-start.9
  850.9 1.9 copy-start.12
  858.5 13.1 %copy-start.1 = (bf16[1024,1024]{0,1:T(8,128)(2,1)S(1)}, bf16[1024,1024]{0,1:T(8,128)(2,1)}, u32[]{:S(2)}) copy-start(bf16[1024,1024]{0,1:T(8,128)(2,1)} %all-reduce.5.cloned.1.call-done) | copy-start | bytes 6291460
  871.6 14.2 %copy-start.7 = (f32[1024]{0:T(1024)S(1)}, f32[1024]{0:T(1024)}, u32[]{:S(2)}) copy-start(f32[1024]{0:T(1024)} %copy-done.6) | copy-start | bytes 12292
  871.6 14.2 %copy-start.2 = (f32[1024,1024]{0,1:T(8,128)S(1)}, f32[1024,1024]{0,1:T(8,128)}, u32[]{:S(2)}) copy-start(f32[1024,1024]{0,1:T(8,128)} %all-reduce.7.cloned.1.call-done) | copy-start | bytes 12582916
  871.6 14.2 %copy-start.3 = (bf16[1024,1024]{0,1:T(8,128)(2,1)S(1)}, bf16[1024,1024]{0,1:T(8,128)(2,1)}, u32[]{:S(2)}) copy-start(bf16[1024,1024]{0,1:T(8,128)(2,1)} %get-tuple-element.17) | copy-start | bytes 6291460
  871.6 14.2 %copy-start.16 = (pred[1024]{0:T(1024)(128)(4,1)S(1)}, pred[1024]{0:T(1024)(128)(4,1)}, u32[]{:S(2)}) copy-start(pred[1024]{0:T(1024)(128)(4,1)} %copy-done.15) | copy-start | bytes 3076
  889.8 5.4 copy-start.10
  906.7 10.6 %copy-start.13 = (f32[1,1024]{1,0:T(1,128)S(1)}, f32[1,1024]{1,0:T(1,128)}, u32[]{:S(2)}) copy-start(f32[1,1024]{1,0:T(1,128)} %get-tuple-element.13) | copy-start | bytes 12292
  916.0 6.4 collective-permute-start
Sparse Core Ops, SparseCore 0:
  9.6 16.1 all-gather.11
  40.2 132.5 all-reduce.4
  174.4 23.2 all-gather.7
  199.2 24.8 all-gather.5
  225.6 24.8 all-gather.9
  582.4 188.9 all-reduce.6
  815.3 26.3 reduce-scatter.5
  844.6 28.5 reduce-scatter.7
  876.2 28.5 reduce-scatter.9
where the time goes:
time: 945 us; the launch traced here: 936 us
  waiting for transfers between devices  383 us (41%)
  blocking collectives  309 us (33%)
  matrix products  170 us (18%)
  other arithmetic  29 us (3%)
  local copies, waits for them, and re-layouts  26.1 us (3%)
  between operations  17 us (2%)
    psum x1, waiting for transfers between devices, device_step(): lax.psum(jnp.einsum('tv,vd->td', d_logits, table_part, preferred_element_...  189 us
    pmax x1, blocking collectives, device_step(): row_max = lax.pmax(jnp.max(logits, axis=-1), 'model')  151 us
    psum x1, blocking collectives, device_step(): tok_stats = lax.psum(part_stats, 'model')  146 us
    psum x1, waiting for transfers between devices, device_step(): x_emb = lax.psum(emb_rows, 'model').astype(jnp.float32)  131 us
    dot_general x1, matrix products, mlp_backward(): jnp.einsum('td,fd->tf', d_mlp, w_down, preferred_element_type=jnp.float32)  25.4 us
    all_gather x1, waiting for transfers between devices, device_step(): w_up = lax.all_gather(up_shard, 'fsdp', axis=0, tiled=True)  22.3 us
    dot_general x1, matrix products, mlp_backward(): jnp.einsum('tf,td->fd', act_bf, d_mlp, preferred_element_type=jnp.float32)  21 us
  transfers between devices with their start and end apart: 10, of which 6 were waited for; matrix products, arithmetic and copies ran while one was open for 15% of the time, Pallas kernels for 0%

commit v1 on v0

v1 whole, which is shorter than its diff:
```python
import functools
import itertools

import jax
import jax.numpy as jnp
from jax import lax
from jax.experimental import pallas as pl
from jax.experimental.pallas import tpu as pltpu
from jax.sharding import PartitionSpec as P

EPS = 1e-6
MESH = pl.DeviceIdType.MESH
VMEM_LIMIT = 67043328
F32 = jnp.float32
BF16 = jnp.bfloat16
COLORS = 3
DIRECT = 3
PARTS = 8
RING = 4
TOP, SUM, LABEL = range(3)


def contract(a, b, dims):
    return lax.dot_general(a, b, (dims, ((), ())), preferred_element_type=F32)


def nn(a, b):
    return contract(a, b, ((1,), (0,)))


def nt(a, b):
    return contract(a, b, ((1,), (1,)))


def tn(a, b):
    return contract(a, b, ((0,), (0,)))


def span(i, n):
    return pl.ds(pl.multiple_of(i * n, n), n)


def loop(lo, hi, body):
    def step(i, carry):
        body(i)
        return carry

    lax.fori_loop(lo, hi, step, 0)


def mean(v):
    return jnp.mean(v, axis=-1, keepdims=True)


def rms_scale(values, gain):
    return values * lax.rsqrt(mean(values * values) + EPS) * gain


def rms_back(values, gain, grad):
    r = lax.rsqrt(mean(values * values) + EPS)
    gg = grad * gain
    return r * gg - values * (r * r * r) * mean(values * gg)


def one_hot(rows, ids):
    return (lax.broadcasted_iota(jnp.int32, (rows, ids.shape[-1]), 0) == ids).astype(F32).astype(BF16)


class Local:
    def __init__(self, sems):
        self.sems, self.free = sems, itertools.count()

    def __call__(self, src, dst):
        return pltpu.make_async_copy(src, dst, self.sems.at[next(self.free)])


class Cube:
    def __init__(self, model, rows, width):
        axes = 1
        while RING**axes < model:
            axes += 1
        self.axes, self.nb, self.rows = axes, 2 * axes, rows
        self.direct = min(DIRECT, self.nb - 1)
        self.walk = self.nb - self.direct
        self.peers = 2**self.direct - 1
        self.last = rows >> self.nb
        tiles = width // 128
        big = -(-tiles // COLORS) * 128
        self.widths = [big, big, width - 2 * big]
        self.starts = [0, big, 2 * big]

    def dim(self, k, s):
        d = (k + s) % self.nb
        return d % self.axes, d // self.axes

    def bind(self, psend=None, precv=None):
        self.m = lax.axis_index("model")
        self.c = lax.axis_index("fsdp")
        self.psend, self.precv, self.free = psend, precv, itertools.count()
        self.digits = [(self.m // RING**a) % RING for a in range(self.axes)]
        self.bit, self.base = [], []
        for k in range(COLORS):
            bits, bases = [], [0]
            for s in range(self.nb):
                a, kind = self.dim(k, s)
                b = self.digits[a]
                v0, v1 = (b % 2 + b // 2) % 2, b // 2
                bits.append(v0 + ((kind + self.c) % 2) * (v1 - v0))
                bases.append(bases[-1] + bits[-1] * (self.rows >> len(bits)))
            self.bit.append(bits)
            self.base.append(bases)

    def toggled(self, k, steps):
        digits = list(self.digits)
        for s in steps:
            a, kind = self.dim(k, s)
            near = 1 - 2 * (digits[a] % 2)
            digits[a] = digits[a] + near + ((kind + self.c) % 2) * (RING - 1 - 2 * digits[a] - near)
        return sum(v * RING**a for a, v in enumerate(digits))

    def group(self, q):
        return [self.walk + i for i in range(self.direct) if (q >> i) % 2]

    def ring_peer(self, a, step):
        b = self.digits[a]
        return self.m + RING**a * ((b + step) % RING - b)

    def barrier(self, rings=False):
        sem = pltpu.get_barrier_semaphore()
        peers = [(self.m, 1 - self.c)]
        for k in range(COLORS):
            steps = [[s] for s in range(self.walk)] + [self.group(q + 1) for q in range(self.peers)]
            peers += [(self.toggled(k, st), self.c) for st in steps]
        if rings:
            peers += [(self.ring_peer(a, step), self.c) for a in range(self.axes) for step in range(1, RING)]
        for peer in peers:
            pl.semaphore_signal(sem, inc=1, device_id=peer, device_id_type=MESH)
        pl.semaphore_wait(sem, len(peers))

    def place(self, k, j):
        pos = []
        for c in range(2):
            p = 0
            for s in range(self.nb):
                a, kind = self.dim(k, s)
                p = 2 * p + (j >> (a + self.axes * ((kind + c) % 2))) % 2
            pos.append(p * self.last)
        return self.rows_at(pos[0] + self.c * (pos[1] - pos[0]), self.last)

    def rows_at(self, start, size):
        return pl.ds(pl.multiple_of(start, self.last), size)

    def cols(self, k):
        return pl.ds(self.starts[k], self.widths[k])

    def pieces(self):
        return itertools.product(range(2**self.nb), range(COLORS))

    def spread(self, nat, bufs):
        for j, k in self.pieces():
            bufs[k][self.place(k, j), :] = nat[span(j, self.last), self.cols(k)]

    def collect(self, bufs, nat, half=None):
        start = 0 if half is None else half * self.rows
        for j, k in self.pieces():
            nat[self.rows_at(start + j * self.last, self.last), self.cols(k)] = bufs[k][self.place(k, j), :]

    def own(self, k):
        return self.rows_at(self.base[k][-1], self.last)

    def put_own(self, bufs, value):
        for k in range(COLORS):
            bufs[k][self.own(k), :] = value[:, self.starts[k] : self.starts[k] + self.widths[k]]

    def get_own(self, bufs):
        return jnp.concatenate([bufs[k][self.own(k), :] for k in range(COLORS)], axis=1)

    def send(self, src, dst, sems, index, peer):
        return pltpu.make_async_remote_copy(
            src_ref=src, dst_ref=dst, send_sem=sems[0].at[index], recv_sem=sems[1].at[index], device_id=(peer, self.c), device_id_type=MESH
        )

    def rs_copies(self, bufs, recvs, sems, k, s):
        if s < self.walk:
            ln = self.rows >> (s + 1)
            start = self.base[k][s] + (1 - self.bit[k][s]) * ln
            off = self.rows - (self.rows >> s)
            peer = self.toggled(k, [s])
            return [self.send(bufs[k].at[self.rows_at(start, ln)], recvs[k].at[pl.ds(off, ln)], sems, (k, s), peer)]
        out = []
        for q in range(self.peers):
            steps = self.group(q + 1)
            start = self.base[k][-1] + sum((1 - 2 * self.bit[k][st]) * (self.rows >> (st + 1)) for st in steps)
            src = bufs[k].at[self.rows_at(start, self.last)]
            out.append(self.send(src, recvs[k].at[self.slot(q)], sems, (k, s + q), self.toggled(k, steps)))
        return out

    def slot(self, q):
        return pl.ds(self.rows - (self.rows >> self.walk) + q * self.last, self.last)

    def rs_add(self, bufs, recvs, k, s):
        if s < self.walk:
            ln = self.rows >> (s + 1)
            at = self.rows_at(self.base[k][s + 1], ln)
            got = recvs[k][pl.ds(self.rows - (self.rows >> s), ln), :].astype(F32)
        else:
            at = self.own(k)
            got = sum(recvs[k][self.slot(q), :].astype(F32) for q in range(self.peers))
        bufs[k][at, :] = (bufs[k][at, :].astype(F32) + got).astype(bufs[k].dtype)

    def reduce_scatter(self, bufs, recvs, sems, fill=None):
        for k in range(COLORS):
            self.start(self.rs_copies(bufs, recvs, sems, k, 0))
        for s in range(self.walk + 1):
            if fill is not None:
                fill(s)
            for k in range(COLORS):
                self.finish(self.rs_copies(bufs, recvs, sems, k, s))
                self.rs_add(bufs, recvs, k, s)
                if s < self.walk:
                    self.start(self.rs_copies(bufs, recvs, sems, k, s + 1))

    def start(self, copies):
        for copy in copies:
            copy.start()

    def finish(self, copies):
        for copy in copies:
            copy.wait()

    def ag_copies(self, bufs, sems, k, s):
        if s == self.walk:
            ref = bufs[k].at[self.own(k)]
            return [self.send(ref, ref, sems, (k, s + q), self.toggled(k, self.group(q + 1))) for q in range(self.peers)]
        ref = bufs[k].at[self.rows_at(self.base[k][s + 1], self.rows >> (s + 1))]
        return [self.send(ref, ref, sems, (k, s), self.toggled(k, [s]))]

    def ag_start(self, bufs, sems):
        for k in range(COLORS):
            self.start(self.ag_copies(bufs, sems, k, self.walk))
        return self.walk

    def ag_next(self, bufs, sems, s):
        for k in range(COLORS):
            self.finish(self.ag_copies(bufs, sems, k, s))
            if s > 0:
                self.start(self.ag_copies(bufs, sems, k, s - 1))
        return s - 1

    def all_gather(self, bufs, sems, fill=None):
        s = self.ag_start(bufs, sems)
        while s >= 0:
            if fill is not None:
                fill(s)
            s = self.ag_next(bufs, sems, s)

    def pair(self, src, dst):
        i = next(self.free)
        return pltpu.make_async_remote_copy(
            src_ref=src, dst_ref=dst, send_sem=self.psend.at[i], recv_sem=self.precv.at[i], device_id=(self.m, 1 - self.c), device_id_type=MESH
        )

    def groups(self, *dtypes):
        return [pltpu.VMEM((self.rows, w), dtype) for dtype in dtypes for w in self.widths]

    def sems(self, n):
        return [pltpu.SemaphoreType.DMA((COLORS, self.walk + self.peers))] * (2 * n)


def by(n, items):
    return [items[i : i + n] for i in range(0, len(items), n)]


def embed_kernel(cube, vb, idx, e_ref, wg, wu, wd, g1, g2, hn, ep_o, wgh_o, wuh_o, h_own, gt_own, u_own, x_own, *scratch):
    wd_s, ep, wgh, wuh, xnat, x32, mp, mr, psend, precv, lsem, *rest = scratch
    xb, xr, hb = by(COLORS, rest[: 3 * COLORS])
    rs_sems, hg_sems = by(2, rest[3 * COLORS :])
    cube.bind(psend, precv)
    local = Local(lsem)
    c = cube.c
    d = hn.shape[1]
    half_d, half_f = d // 2, wgh.shape[1]
    last = cube.last
    mine_d = span(c, half_d)
    e_local = local(e_ref, ep.at[pl.ds(0, vb)])
    e_local.start()
    w_local = [local(wd, wd_s), local(wg.at[:, span(c, half_f)], wgh.at[mine_d]), local(wu.at[:, span(c, half_f)], wuh.at[mine_d])]
    cube.barrier()
    e_pair = cube.pair(e_ref, ep.at[pl.ds(vb, vb)])
    e_pair.start()
    w_pair = [cube.pair(src.at[:, span(1 - c, half_f)], dst.at[mine_d]) for src, dst in ((wg, wgh), (wu, wuh))]
    cube.start(w_pair + w_local)
    cube.finish([e_local, e_pair])
    outs = [local(ep, ep_o), local(wgh, wgh_o), local(wuh, wuh_o)]
    outs[0].start()
    chunk = min(256, cube.rows)

    def lookup(i):
        at = span(i, chunk)
        xnat[at, :] = tn(one_hot(2 * vb, idx[:, at]), ep[...]).astype(BF16)

    loop(0, cube.rows // chunk, lookup)
    cube.spread(xnat, xb)
    cube.reduce_scatter(xb, xr, rs_sems)
    x_own[...] = cube.get_own(xb)
    x32[0] = x_own[...]
    x_pair = cube.pair(x32.at[0], x32.at[1])
    x_pair.start()
    cube.finish(w_local + w_pair)
    cube.start(outs[1:])
    x_pair.wait()
    a_rows = rms_scale(x32[...].reshape(2 * last, d).astype(F32), g1[...]).astype(BF16)
    parts = 4
    fc = half_f // parts
    total = jnp.zeros((2 * last, d), F32)
    for p in range(parts):
        at = pl.ds(p * fc, fc)
        gate = nn(a_rows, wgh[:, at]).astype(BF16)
        up = nn(a_rows, wuh[:, at]).astype(BF16)
        gt_own[:, at] = gate
        u_own[:, at] = up
        gate_f = gate.astype(F32)
        act = (gate_f * jax.nn.sigmoid(gate_f) * up.astype(F32)).astype(BF16)
        total = total + nn(act, wd_s[at, :])
    mp[...] = total.reshape(2, last, d)
    m_pair = cube.pair(mp.at[1], mr)
    m_pair.start()
    m_pair.wait()
    h_rows = x_own[...].astype(F32) + (mp[0] + mr[...]).astype(BF16).astype(F32)
    h_own[...] = h_rows
    cube.put_own(hb, rms_scale(h_rows, g2[...]).astype(BF16))
    cube.all_gather(hb, hg_sems)
    cube.collect(hb, hn)
    cube.finish(outs)


def head_kernel(
    cube, vb, real, num_tokens, hn, ep, lab, h_own, g2, x_own, g1, gt_own, u_own, wgh_i, wuh_i, wd_i,
    dmf, loss, deh, dx_own, at_o, gt_o, u_o, *scratch
):
    z, dz, nat, stats, lbuf, dm32, mp, mr, wgh, wuh, wd, xf, tstage, stage, psend, precv, lsem, osem, st_s, st_r, *rest = scratch
    rb, rr, gb, xg = by(COLORS, rest[: 4 * COLORS])
    rs_sems, ag_sems, xg_sems = by(2, rest[4 * COLORS :])
    cube.bind(psend, precv)
    local = Local(lsem)
    c = cube.c
    t, d = hn.shape
    walk, last = cube.walk, cube.last
    w_copies = [local(wgh_i, wgh), local(wuh_i, wuh), local(wd_i, wd)]
    cube.start(w_copies)
    cube.put_own(xg, x_own[...])
    cube.barrier(rings=True)
    xstep = cube.ag_start(xg, xg_sems)
    chunk = min(256, t)
    chunks = t // chunk
    mine = cube.digits[0]

    def logits(i):
        at = span(i, chunk)
        row = lax.broadcasted_iota(jnp.int32, (2 * vb, chunk), 0)
        valid = (row < real) | ((row >= vb) & (row < vb + real))
        zz = jnp.where(valid, nt(ep[...], hn[at, :]), -1e38)
        z[:, at] = zz
        top = jnp.max(zz, axis=0, keepdims=True)
        parts = {TOP: top, SUM: jnp.exp(zz - top), LABEL: jnp.where(row == lab[:, at], zz, 0.0)}
        for r, v in parts.items():
            stats[0, mine, pl.ds(r, 1), at] = v if r == TOP else jnp.sum(v, axis=0, keepdims=True)

    loop(0, chunks, logits)
    xstep = cube.ag_next(xg, xg_sems, xstep)
    for a in range(cube.axes):
        here = stats.at[a, cube.digits[a]]
        copies = [cube.send(here, here, (st_s, st_r), (a, step - 1), cube.ring_peer(a, step)) for step in range(1, RING)]
        cube.start(copies)
        cube.finish(copies)
        if xstep > 1:
            xstep = cube.ag_next(xg, xg_sems, xstep)
        tops, sums, labels = [[stats[a, i, pl.ds(r, 1), :] for i in range(RING)] for r in range(LABEL + 1)]
        top = functools.reduce(jnp.maximum, tops)
        total = sum(v * jnp.exp(m - top) for m, v in zip(tops, sums))
        label = sum(labels)
        slot = cube.digits[a + 1] if a + 1 < cube.axes else 0
        for r, v in enumerate((top, total, label)):
            stats[a + 1, slot, pl.ds(r, 1), :] = v
    while xstep > 0:
        xstep = cube.ag_next(xg, xg_sems, xstep)
    tok_loss = jnp.sum(top + jnp.log(total) - label, axis=1, keepdims=True)
    lbuf[c] = jnp.broadcast_to(tok_loss, lbuf.shape[1:])
    l_pair = cube.pair(lbuf.at[c], lbuf.at[c])
    l_pair.start()
    final = stats.at[cube.axes, 0]

    def backward(i):
        at = span(i, chunk)
        row = lax.broadcasted_iota(jnp.int32, (2 * vb, chunk), 0)
        soft = jnp.exp(z[:, at] - final[pl.ds(TOP, 1), at]) / final[pl.ds(SUM, 1), at]
        dzz = (jnp.where(row == lab[:, at], soft - 1.0, soft) / num_tokens).astype(BF16)
        dz[:, at] = dzz
        nat[at, :] = tn(dzz, ep[...])

    loop(0, chunks, backward)
    cube.spread(nat, rb)
    mine_t = span(c, t)
    xf_pair = cube.pair(xf.at[mine_t], xf.at[mine_t])
    dm_pair = cube.pair(dmf.at[mine_t], dmf.at[mine_t])
    d_pair = cube.pair(dm32.at[0], dm32.at[1])
    m_pair = cube.pair(mp.at[1], mr)
    t_out = local(tstage, at_o)
    fc = wgh.shape[1] // PARTS
    tile = min(512, 2 * t)

    def out_copies(p):
        return [pltpu.make_async_copy(stage.at[p % 2, i], dst.at[p], osem.at[i, p]) for i, dst in enumerate((gt_o, u_o))]

    def gate_up(p):
        if p >= 2:
            cube.finish(out_copies(p - 2))
        cols = pl.ds(p * fc, fc)
        slot = stage.at[p % 2]

        def body(i):
            at = span(i, tile)
            for which, w in enumerate((wgh, wuh)):
                slot[which, at, :] = nn(xf[at, :], w[:, cols]).astype(BF16)

        loop(0, 2 * t // tile, body)
        cube.start(out_copies(p))

    def normalise():
        def body(i):
            at = span(i, chunk)
            val = rms_scale(xf[at, :].astype(F32), g1[...])
            xf[at, :] = val.astype(BF16)
            tstage[:, at] = val.T.astype(BF16)

        loop(0, 2 * chunks, body)

    def head_grad(i):
        deh[span(i, vb), :] = nn(dz[span(i, vb), :], hn[...])

    todo = list(range(PARTS))

    def run(n):
        while n > 0 and todo:
            gate_up(todo.pop(0))
            n -= 1

    def rs_fill(s):
        if s == 0:
            loop(0, 2, head_grad)
            cube.ag_next(xg, xg_sems, xstep)
            cube.collect(xg, xf, c)
            xf_pair.start()
            cube.finish(w_copies + [xf_pair])
            normalise()
            t_out.start()
            run(1)
        else:
            run(walk + 1 - s)

    cube.reduce_scatter(rb, rr, rs_sems, rs_fill)
    dh = rms_back(h_own[...], g2[...], cube.get_own(rb))
    dm = dh.astype(BF16)
    cube.put_own(gb, dm)
    dm32[0] = dm

    def token_back():
        d_pair.wait()
        w = wgh.shape[1] // RING
        part = jnp.zeros((2 * last, d), F32)
        for p in range(RING):
            at = pl.ds(p * w, w)
            d_act = nt(dm32[...].reshape(2 * last, d), wd[at, :])
            gate = gt_own[:, at].astype(F32)
            sig = jax.nn.sigmoid(gate)
            d_gate = (d_act * u_own[:, at].astype(F32) * (sig * (1.0 + gate * (1.0 - sig)))).astype(BF16)
            d_up = (d_act * (gate * sig)).astype(BF16)
            part = part + (nt(d_gate, wgh[:, at]) + nt(d_up, wuh[:, at]))
        mp[...] = part.reshape(mp.shape)
        m_pair.start()

    def ag_fill(s):
        if s == walk:
            token_back()
        else:
            run(1)

    d_pair.start()
    cube.all_gather(gb, ag_sems, ag_fill)
    cube.collect(gb, dmf, c)
    dm_pair.start()
    run(PARTS)
    m_pair.wait()
    dx_own[...] = dh + rms_back(x_own[...].astype(F32), g1[...], mp[0] + mr[...])
    l_pair.wait()
    loss[...] = (lbuf[0] + lbuf[1]) / num_tokens
    t_out.wait()
    cube.finish(out_copies(PARTS - 2) + out_copies(PARTS - 1) + [dm_pair])


def table_kernel(cube, vb, idx, dx_own, dmf, wd, deh, at_i, gt_i, u_i, de, act_o, dg_o, du_o, got_g, got_u, *scratch):
    nat, mix, de_r, aoth, fin, fout, part, psend, precv, lsem, isem, osem, gsend, grecv, *rest = scratch
    gb, ag_sems = rest[:COLORS], rest[COLORS:]
    cube.bind(psend, precv)
    c = cube.c
    t = cube.rows
    fc = wd.shape[0] // PARTS
    half_d = aoth.shape[0]
    a_copy = pltpu.make_async_copy(at_i.at[span(1 - c, half_d)], aoth, lsem)

    def in_copies(p):
        return [pltpu.make_async_copy(src.at[p], fin.at[p % 2, i], isem.at[i, p]) for i, src in enumerate((gt_i, u_i))]

    def out_copies(p):
        return [pltpu.make_async_copy(fout.at[p % 2, i], dst.at[p], osem.at[i, p]) for i, dst in enumerate((act_o, dg_o, du_o))]

    def send_copies(p):
        dev = (cube.m, 1 - c)
        return [
            pltpu.make_async_remote_copy(
                src_ref=part.at[p % 2, i], dst_ref=dst.at[p], send_sem=gsend.at[i, p], recv_sem=grecv.at[i, p], device_id=dev, device_id_type=MESH
            )
            for i, dst in enumerate((got_g, got_u))
        ]

    def drain(p):
        cube.finish(out_copies(p))
        for copy in send_copies(p):
            copy.wait_send()

    cube.start([a_copy] + in_copies(0))
    cube.put_own(gb, dx_own[...])
    cube.barrier()
    step = cube.ag_start(gb, ag_sems)
    mix[...] = deh[...]
    a_copy.wait()
    tile = min(512, 2 * t)
    for p in range(PARTS):
        if p + 1 < PARTS:
            cube.start(in_copies(p + 1))
        cube.finish(in_copies(p))
        if p >= 2:
            drain(p - 2)
        src, dst, res = fin.at[p % 2], fout.at[p % 2], part.at[p % 2]

        def body(i):
            at = span(i, tile)
            d_act = nt(dmf[at, :], wd[pl.ds(p * fc, fc), :])
            gate = src[0, at, :].astype(F32)
            up = src[1, at, :].astype(F32)
            sig = jax.nn.sigmoid(gate)
            silu = gate * sig
            outs = (silu * up, d_act * up * (sig * (1.0 + gate * (1.0 - sig))), d_act * silu)
            for which, v in enumerate(outs):
                dst[which, at, :] = v.astype(BF16)

        loop(0, 2 * t // tile, body)
        for which in range(2):
            res[which] = nn(aoth[...], dst[which + 1])
        cube.start(out_copies(p) + send_copies(p))
        if step > 0 and p % 2 < 1:
            step = cube.ag_next(gb, ag_sems, step)
    while step >= 0:
        step = cube.ag_next(gb, ag_sems, step)
    cube.collect(gb, nat)
    chunk = min(256, t)

    def scatter(i):
        at = span(i, chunk)
        hot = one_hot(2 * vb, idx[:, at])
        val = nat[at, :]
        hi = val.astype(BF16)
        rest = val - hi.astype(F32)
        mid = rest.astype(BF16)
        low = (rest - mid.astype(F32)).astype(BF16)
        mix[...] = mix[...] + ((nn(hot, low) + nn(hot, mid)) + nn(hot, hi))

    loop(0, t // chunk, scatter)
    e_pair = cube.pair(mix.at[pl.ds(vb, vb)], de_r)
    e_pair.start()
    drain(PARTS - 2)
    drain(PARTS - 1)
    for p in range(PARTS):
        for copy in send_copies(p):
            copy.wait_recv()
    e_pair.wait()
    de[...] = mix[pl.ds(0, vb), :] + de_r[...]


def weight_kernel(core, aown, dg, du, act, dmf, got_g, got_u, og, ou, od):
    even = pl.program_id(0) % 2 == 0
    n, _, fc = dg.shape

    @pl.when(even)
    def _():
        for i in range(n):
            og[:, pl.ds(i * fc, fc)] = nn(aown[...], dg[i])
            ou[:, pl.ds(i * fc, fc)] = nn(aown[...], du[i])

    @pl.when(jnp.logical_not(even))
    def _():
        for i in range(n):
            og[:, pl.ds(i * fc, fc)] = got_g[i]
            ou[:, pl.ds(i * fc, fc)] = got_u[i]
            od[pl.ds(i * fc, fc), :] = tn(act[i], dmf[...])


def solution(mesh):
    model, fsdp_size = mesh.shape["model"], mesh.shape["fsdp"]
    tok_spec = P("fsdp", None)
    row_spec = P(("model", "fsdp"), None)
    weight_spec = P("fsdp", None)
    vmem = pl.BlockSpec(memory_space=pltpu.VMEM)
    hbm = pl.BlockSpec(memory_space=pl.ANY)
    sds = jax.ShapeDtypeStruct
    dma = pltpu.SemaphoreType.DMA

    def params(cid):
        return pltpu.CompilerParams(collective_id=cid, has_side_effects=True, vmem_limit_bytes=VMEM_LIMIT)

    def device_step(tok_ids, tok_labels, table_shard, gate_shard, up_shard, down_shard, gain_in, gain_out):
        t = tok_ids.size
        num_tokens = t * fsdp_size
        real, d = table_shard.shape
        vb = -(-real // 16) * 16
        f = gate_shard.shape[1]
        half_f, half_d = f // 2, d // 2
        fc = half_f // PARTS
        cube = Cube(model, t, d)
        last = cube.last
        me, core = lax.axis_index("model"), lax.axis_index("fsdp")
        first = (2 * me + core) * real
        other = (2 * me + 1 - core) * real

        def local_rows(ids):
            flat = ids.reshape(1, t)
            here, there = flat - first, flat - other
            return jnp.where((here >= 0) & (here < real), here, jnp.where((there >= 0) & (there < real), vb + there, -1))

        idx = local_rows(tok_ids)
        lab = local_rows(tok_labels)
        table = jnp.pad(table_shard, ((0, vb - real), (0, 0)))
        g1, g2 = gain_in.reshape(1, d), gain_out.reshape(1, d)
        act_own = sds((2 * last, half_f), BF16)
        w_half = sds((d, half_f), BF16)
        hn, ep, wgh, wuh, h_own, gt_own, u_own, x_own = pl.pallas_call(
            functools.partial(embed_kernel, cube, vb),
            out_shape=(sds((t, d), BF16), sds((2 * vb, d), BF16), w_half, w_half, sds((last, d), F32), act_own, act_own, sds((last, d), BF16)),
            in_specs=[vmem, hbm, hbm, hbm, hbm, vmem, vmem],
            out_specs=(vmem, hbm, hbm, hbm, vmem, vmem, vmem, vmem),
            scratch_shapes=[
                pltpu.VMEM((half_f, d), BF16),
                pltpu.VMEM((2 * vb, d), BF16),
                pltpu.VMEM((d, half_f), BF16),
                pltpu.VMEM((d, half_f), BF16),
                pltpu.VMEM((t, d), BF16),
                pltpu.VMEM((2, last, d), BF16),
                pltpu.VMEM((2, last, d), F32),
                pltpu.VMEM((last, d), F32),
                dma((8,)),
                dma((8,)),
                dma((8,)),
            ]
            + cube.groups(BF16, BF16, BF16)
            + cube.sems(2),
            compiler_params=params(0),
            name="embed",
        )(idx, table, gate_shard, up_shard, down_shard, g1, g2)
        chunked = sds((PARTS, 2 * t, fc), BF16)
        dmf, loss, deh, dx_own, a_t, gt, u = pl.pallas_call(
            functools.partial(head_kernel, cube, vb, real, num_tokens),
            out_shape=(sds((2 * t, d), BF16), sds((8, 128), F32), sds((2 * vb, d), F32), sds((last, d), F32), sds((d, 2 * t), BF16), chunked, chunked),
            in_specs=[vmem] * 9 + [hbm] * 3,
            out_specs=(vmem,) * 4 + (hbm,) * 3,
            scratch_shapes=[
                pltpu.VMEM((2 * vb, t), F32),
                pltpu.VMEM((2 * vb, t), BF16),
                pltpu.VMEM((t, d), F32),
                pltpu.VMEM((cube.axes + 1, RING, RING, t), F32),
                pltpu.VMEM((2, 8, 128), F32),
                pltpu.VMEM((2, last, d), BF16),
                pltpu.VMEM((2, last, d), F32),
                pltpu.VMEM((last, d), F32),
                pltpu.VMEM((d, half_f), BF16),
                pltpu.VMEM((d, half_f), BF16),
                pltpu.VMEM((half_f, d), BF16),
                pltpu.VMEM((2 * t, d), BF16),
                pltpu.VMEM((d, 2 * t), BF16),
                pltpu.VMEM((2, 2, 2 * t, fc), BF16),
                dma((8,)),
                dma((8,)),
                dma((8,)),
                dma((2, PARTS)),
                dma((cube.axes, RING)),
                dma((cube.axes, RING)),
            ]
            + cube.groups(F32, F32, BF16, BF16)
            + cube.sems(3),
            compiler_params=params(1),
            name="head",
        )(hn, ep, lab, h_own, g2, x_own, g1, gt_own, u_own, wgh, wuh, down_shard)
        got = sds((PARTS, half_d, fc), F32)
        de, act, d_gate, d_up, got_g, got_u = pl.pallas_call(
            functools.partial(table_kernel, cube, vb),
            out_shape=(sds((vb, d), F32), chunked, chunked, chunked, got, got),
            in_specs=[vmem] * 5 + [hbm] * 3,
            out_specs=(vmem,) + (hbm,) * 5,
            scratch_shapes=[
                pltpu.VMEM((t, d), F32),
                pltpu.VMEM((2 * vb, d), F32),
                pltpu.VMEM((vb, d), F32),
                pltpu.VMEM((half_d, 2 * t), BF16),
                pltpu.VMEM((2, 2, 2 * t, fc), BF16),
                pltpu.VMEM((2, 3, 2 * t, fc), BF16),
                pltpu.VMEM((2, 2, half_d, fc), F32),
                dma((1,)),
                dma((1,)),
                dma,
                dma((2, PARTS)),
                dma((3, PARTS)),
                dma((2, PARTS)),
                dma((2, PARTS)),
            ]
            + cube.groups(F32)
            + cube.sems(1),
            compiler_params=params(2),
            name="table",
        )(idx, dx_own, dmf, down_shard, deh, a_t, gt, u)
        wide = 2
        chunk_spec = pl.BlockSpec((wide, 2 * t, fc), lambda i, s: (i // 2, 0, 0))
        got_spec = pl.BlockSpec((wide, half_d, fc), lambda i, s: (i // 2, 0, 0))
        grad_spec = pl.BlockSpec((half_d, wide * fc), lambda i, s: (0, (s[0] + i % 2) % 2 * (PARTS // wide) + i // 2))
        grad_gate, grad_up, grad_down = pl.pallas_call(
            weight_kernel,
            out_shape=(sds((half_d, f), F32), sds((half_d, f), F32), sds((half_f, d), F32)),
            grid_spec=pltpu.PrefetchScalarGridSpec(
                num_scalar_prefetch=1,
                grid=(2 * PARTS // wide,),
                in_specs=[
                    pl.BlockSpec((half_d, 2 * t), lambda i, s: (s[0], 0)),
                    chunk_spec,
                    chunk_spec,
                    chunk_spec,
                    pl.BlockSpec((2 * t, d), lambda i, s: (0, 0)),
                    got_spec,
                    got_spec,
                ],
                out_specs=(grad_spec, grad_spec, pl.BlockSpec((wide * fc, d), lambda i, s: (i // 2, 0))),
            ),
            compiler_params=pltpu.CompilerParams(vmem_limit_bytes=VMEM_LIMIT),
            name="weights",
        )(core.reshape(1).astype(jnp.int32), a_t, d_gate, d_up, act, dmf, got_g, got_u)
        return loss[0, 0], de[:real], grad_gate, grad_up, grad_down

    return jax.shard_map(device_step, mesh=mesh, in_specs=(tok_spec, tok_spec, row_spec, weight_spec, weight_spec, weight_spec, P(), P()), out_specs=(P(), row_spec, weight_spec, weight_spec, weight_spec), check_vma=False)
```

time: 945 us -> 256 us (0.27)
  waiting for transfers between devices: 383 us -> 0 us
  blocking collectives: 309 us -> 0 us
  Pallas kernels: 0 us -> 248 us
  matrix products: 170 us -> 0 us
  other arithmetic: 29 us -> 1.33 us
  local copies, waits for them, and re-layouts: 26.1 us -> 6.06 us
  between operations: 17 us -> 0.67 us
    psum x2 -> x0, waiting for transfers between devices: 320 us -> none  [the longest x1 189 us: device_step(): lax.psum(jnp.einsum('tv,vd->td', d_logits, table_part, preferred_element_...]
    pallas_call x0 -> x4, Pallas kernels: none -> 248 us  [the longest x1 97.1 us: device_step(): pl.pallas_call(functools.partial(head_kernel, cube, vb, real, num_tokens)...]
    dot_general x12 -> x0, matrix products: 170 us -> none  [the longest x1 25.4 us: mlp_backward(): jnp.einsum('td,fd->tf', d_mlp, w_down, preferred_element_type=jnp.float32)]
    pmax x1 -> x0, blocking collectives: 151 us -> none  [device_step(): row_max = lax.pmax(jnp.max(logits, axis=-1), 'model')]
    psum x2 -> x0, blocking collectives: 150 us -> none  [the longest x1 146 us: device_step(): tok_stats = lax.psum(part_stats, 'model')]
    all_gather x4 -> x0, waiting for transfers between devices: 61.3 us -> none  [the longest x1 22.3 us: device_step(): w_up = lax.all_gather(up_shard, 'fsdp', axis=0, tiled=True)]
    scatter-add x1 -> x0, other arithmetic: 11.5 us -> none  [device_step(): jax.ops.segment_sum(jnp.where(id_inside[:, None], d_x, 0.0), safe_ids, nu...]
  transfers between devices with their start and end apart: 10 -> 0, of which waited for: 6 -> 0; matrix products, arithmetic and copies ran while one was open for 15% -> 0% of each run, Pallas kernels for 0% -> 0%
where the time goes in v1:
time: 256 us
  Pallas kernels  248 us (97%)
  local copies, waits for them, and re-layouts  6.06 us (2%)
    pallas_call x1, Pallas kernels, device_step(): pl.pallas_call(functools.partial(head_kernel, cube, vb, real, num_tokens)...  97.1 us
    pallas_call x1, Pallas kernels, device_step(): pl.pallas_call(functools.partial(embed_kernel, cube, vb), out_shape=(sds(...  61.9 us
    pallas_call x1, Pallas kernels, device_step(): pl.pallas_call(functools.partial(table_kernel, cube, vb), out_shape=(sds(...  52.5 us
    pallas_call x1, Pallas kernels, device_step(): pl.pallas_call(weight_kernel, out_shape=(sds((half_d, f), F32), sds((half...  36.3 us

profile of v1, /device:TPU:1, one launch (start us, length us, event | category | flops | bytes accessed | tf_op | source)
XLA Modules:
  0.0 255.8 jit_solution(5520164151909952722)
XLA Ops:
  0.6 1.3 and_select_fusion.1
  2.0 2.1 pad.4.e_ref
  4.1 61.9 %embed.1 = (bf16[1024,1024]{1,0:T(8,128)(2,1)}, bf16[800,1024]{1,0:T(8,128)(2,1)}, bf16[1024,2048]{1,0:T(8,128)(2,1)}, bf16[1024,2048]{1,0:T(8,128)(2,1)}, f32[1...) custom-call(s32[1,1024]{1,0:T(1,128)} %get-tuple-element.54.idx, ...), custom_call_target="tpu_custom_call" | custom-call | tf_op jit(solution)/shard_map/embed/pallas_call | solution.py:646
  66.0 97.1 %head.1 = (bf16[2048,1024]{1,0:T(8,128)(2,1)}, f32[8,128]{1,0:T(8,128)}, f32[800,1024]{1,0:T(8,128)}, f32[16,1024]{1,0:T(8,128)}, bf16[1024,2048]{1,0:T(8,128)(2...) custom-call(bf16[1024,1024]{1,0:T(8,128)(2,1)} %get-tuple-element.29.hn, ...), custom_call_target="tpu_custom_call" | custom-call | tf_op jit(solution)/shard_map/head/pallas_call | solution.py:670
  163.1 1.2 slice.6
  164.3 52.5 %table.1 = (f32[400,1024]{1,0:T(8,128)}, bf16[8,2048,256]{2,1,0:T(8,128)(2,1)}, bf16[8,2048,256]{2,1,0:T(8,128)(2,1)}, bf16[8,2048,256]{2,1,0:T(8,128)(2,1)}, f3...) custom-call(s32[1,1024]{1,0:T(1,128)} %get-tuple-element.54.idx, f32[16,1024]{1,0:T(8,128)} %get-tuple-element.38.dx_own, ...), custom_call_target="tpu_custom_call" | custom-call | tf_op jit(solution)/shard_map/table/pallas_call | solution.py:703
  216.7 36.3 %weights.1 = (f32[512,4096]{1,0:T(8,128)}, f32[512,4096]{1,0:T(8,128)}, f32[2048,1024]{1,0:T(8,128)}) custom-call(s32[1]{0:T(128)} %bitcast.3.core, bf16[1024,2048]{1,0:T(8,128)(2,1)} %get-tuple-element.41.at_i.aown, bf16[8,2048,256]{2,1,0:T(8,128)(2,1)} %get-tuple-element.45.dg, bf16[8,2048,256]{2,1,0:T(8,128)(2,1)} %get-tuple-element.46.du, ...), custom_call_target="tpu_custom_call" | custom-call | tf_op jit(solution)/shard_map/weights/pallas_call | solution.py:733
  253.0 2.8 %copy.14 = f32[393,1024]{1,0:T(8,128)} copy(f32[393,1024]{1,0:T(8,128)} %bitcast.5) | data formatting | bytes 3219456

commit v2 on v1

--- a/solution.py
+++ b/solution.py
@@ -64,6 +64,12 @@
 
 def one_hot(rows, ids):
     return (lax.broadcasted_iota(jnp.int32, (rows, ids.shape[-1]), 0) == ids).astype(F32).astype(BF16)
+
+
+def table_rows(cube, real, vb, ids):
+    here = ids - (2 * cube.m + cube.c) * real
+    there = ids - (2 * cube.m + 1 - cube.c) * real
+    return jnp.where((here >= 0) & (here < real), here, jnp.where((there >= 0) & (there < real), vb + there, -1))
 
 
 class Local:
@@ -180,32 +186,42 @@
             src_ref=src, dst_ref=dst, send_sem=sems[0].at[index], recv_sem=sems[1].at[index], device_id=(peer, self.c), device_id_type=MESH
         )
 
-    def rs_copies(self, bufs, recvs, sems, k, s):
-        if s < self.walk:
-            ln = self.rows >> (s + 1)
-            start = self.base[k][s] + (1 - self.bit[k][s]) * ln
-            off = self.rows - (self.rows >> s)
-            peer = self.toggled(k, [s])
-            return [self.send(bufs[k].at[self.rows_at(start, ln)], recvs[k].at[pl.ds(off, ln)], sems, (k, s), peer)]
+    def flip(self, k, steps):
+        return sum((1 - 2 * self.bit[k][s]) * (self.rows >> (s + 1)) for s in steps)
+
+    def start(self, copies):
+        for copy in copies:
+            copy.start()
+
+    def finish(self, copies):
+        for copy in copies:
+            copy.wait()
+
+    def rs_parts(self, k, s):
+        base, off, ln = self.base[k], self.rows - (self.rows >> s), self.rows >> (s + 1)
+        if s == self.walk:
+            first = self.rows - (self.rows >> s)
+            return [(base[-1] + self.flip(k, self.group(q + 1)), base[-1], first + q * self.last, self.last) for q in range(self.peers)]
+        away = base[s + 1] + self.flip(k, [s])
+        if s == self.walk - 1:
+            return [(away, base[s + 1], off, ln)]
+        half = ln // 2
+        b = self.bit[k][s + 1]
+        return [(away + x * half, base[s + 1] + x * half, off + i * half, half) for i, x in enumerate((1 - b, b))]
+
+    def rs_copies(self, bufs, recvs, sems, k, s, which=slice(None)):
         out = []
-        for q in range(self.peers):
-            steps = self.group(q + 1)
-            start = self.base[k][-1] + sum((1 - 2 * self.bit[k][st]) * (self.rows >> (st + 1)) for st in steps)
-            src = bufs[k].at[self.rows_at(start, self.last)]
-            out.append(self.send(src, recvs[k].at[self.slot(q)], sems, (k, s + q), self.toggled(k, steps)))
+        for i, (src, _, dst, ln) in list(enumerate(self.rs_parts(k, s)))[which]:
+            peer = self.toggled(k, self.group(i + 1) if s == self.walk else [s])
+            at = 2 * s + i
+            out.append(self.send(bufs[k].at[self.rows_at(src, ln)], recvs[k].at[pl.ds(dst, ln)], sems, (k, at), peer))
         return out
 
-    def slot(self, q):
-        return pl.ds(self.rows - (self.rows >> self.walk) + q * self.last, self.last)
-
-    def rs_add(self, bufs, recvs, k, s):
-        if s < self.walk:
-            ln = self.rows >> (s + 1)
-            at = self.rows_at(self.base[k][s + 1], ln)
-            got = recvs[k][pl.ds(self.rows - (self.rows >> s), ln), :].astype(F32)
-        else:
-            at = self.own(k)
-            got = sum(recvs[k][self.slot(q), :].astype(F32) for q in range(self.peers))
+    def rs_take(self, bufs, recvs, sems, k, s, which):
+        parts = self.rs_parts(k, s)[which]
+        self.finish(self.rs_copies(bufs, recvs, sems, k, s, which))
+        at = self.rows_at(parts[0][1], parts[0][3])
+        got = sum(recvs[k][pl.ds(dst, ln), :].astype(F32) for _, _, dst, ln in parts)
         bufs[k][at, :] = (bufs[k][at, :].astype(F32) + got).astype(bufs[k].dtype)
 
     def reduce_scatter(self, bufs, recvs, sems, fill=None):
@@ -215,36 +231,45 @@
             if fill is not None:
                 fill(s)
             for k in range(COLORS):
-                self.finish(self.rs_copies(bufs, recvs, sems, k, s))
-                self.rs_add(bufs, recvs, k, s)
+                if 0 < s < self.walk:
+                    self.rs_take(bufs, recvs, sems, k, s - 1, slice(1, 2))
                 if s < self.walk:
+                    self.rs_take(bufs, recvs, sems, k, s, slice(0, 1))
                     self.start(self.rs_copies(bufs, recvs, sems, k, s + 1))
-
-    def start(self, copies):
-        for copy in copies:
-            copy.start()
-
-    def finish(self, copies):
-        for copy in copies:
-            copy.wait()
-
-    def ag_copies(self, bufs, sems, k, s):
-        if s == self.walk:
-            ref = bufs[k].at[self.own(k)]
-            return [self.send(ref, ref, sems, (k, s + q), self.toggled(k, self.group(q + 1))) for q in range(self.peers)]
-        ref = bufs[k].at[self.rows_at(self.base[k][s + 1], self.rows >> (s + 1))]
-        return [self.send(ref, ref, sems, (k, s), self.toggled(k, [s]))]
+                else:
+                    self.rs_take(bufs, recvs, sems, k, s, slice(None))
+
+    def blocks(self, s):
+        later = range(s + 1, self.walk)
+        return [st for n in range(len(later) + 1) for st in itertools.combinations(later, n)]
+
+    def ag_block(self, bufs, sems, k, s, block):
+        at = self.base[k][self.walk] + self.flip(k, block)
+        ref = bufs[k].at[self.rows_at(at, self.rows >> self.walk)]
+        index = 2 ** (self.walk - 1 - s) - 1 + self.blocks(s).index(block)
+        return self.send(ref, ref, sems, (k, self.peers + index), self.toggled(k, [s]))
+
+    def ag_direct(self, bufs, sems, k):
+        ref = bufs[k].at[self.own(k)]
+        return [self.send(ref, ref, sems, (k, q), self.toggled(k, self.group(q + 1))) for q in range(self.peers)]
 
     def ag_start(self, bufs, sems):
         for k in range(COLORS):
-            self.start(self.ag_copies(bufs, sems, k, self.walk))
+            self.start(self.ag_direct(bufs, sems, k))
         return self.walk
 
     def ag_next(self, bufs, sems, s):
-        for k in range(COLORS):
-            self.finish(self.ag_copies(bufs, sems, k, s))
-            if s > 0:
-                self.start(self.ag_copies(bufs, sems, k, s - 1))
+        if s == self.walk:
+            for k in range(COLORS):
+                self.finish(self.ag_direct(bufs, sems, k))
+                for to in range(s - 1, -1, -1):
+                    self.ag_block(bufs, sems, k, to, ()).start()
+            return s - 1
+        for block in self.blocks(s):
+            for k in range(COLORS):
+                self.ag_block(bufs, sems, k, s, block).wait()
+                for to in range(s - 1, -1, -1):
+                    self.ag_block(bufs, sems, k, to, tuple(sorted(block + (s,)))).start()
         return s - 1
 
     def all_gather(self, bufs, sems, fill=None):
@@ -264,15 +289,15 @@
         return [pltpu.VMEM((self.rows, w), dtype) for dtype in dtypes for w in self.widths]
 
     def sems(self, n):
-        return [pltpu.SemaphoreType.DMA((COLORS, self.walk + self.peers))] * (2 * n)
+        return [pltpu.SemaphoreType.DMA((COLORS, self.peers + max(2 * self.walk, 2**self.walk)))] * (2 * n)
 
 
 def by(n, items):
     return [items[i : i + n] for i in range(0, len(items), n)]
 
 
-def embed_kernel(cube, vb, idx, e_ref, wg, wu, wd, g1, g2, hn, ep_o, wgh_o, wuh_o, h_own, gt_own, u_own, x_own, *scratch):
-    wd_s, ep, wgh, wuh, xnat, x32, mp, mr, psend, precv, lsem, *rest = scratch
+def embed_kernel(cube, vb, ids, e_ref, wg, wu, wd, g1, g2, hn, ep_o, wgh_o, wuh_o, h_own, gt_own, u_own, x_own, *scratch):
+    e_s, wd_s, ep, wgh, wuh, xnat, x32, mp, mr, psend, precv, lsem, *rest = scratch
     xb, xr, hb = by(COLORS, rest[: 3 * COLORS])
     rs_sems, hg_sems = by(2, rest[3 * COLORS :])
     cube.bind(psend, precv)
@@ -282,22 +307,30 @@
     half_d, half_f = d // 2, wgh.shape[1]
     last = cube.last
     mine_d = span(c, half_d)
-    e_local = local(e_ref, ep.at[pl.ds(0, vb)])
+    e_local = local(e_ref, e_s)
     e_local.start()
     w_local = [local(wd, wd_s), local(wg.at[:, span(c, half_f)], wgh.at[mine_d]), local(wu.at[:, span(c, half_f)], wuh.at[mine_d])]
     cube.barrier()
-    e_pair = cube.pair(e_ref, ep.at[pl.ds(vb, vb)])
+    e_local.wait()
+    real = e_s.shape[0]
+    body = real - real % 16
+    if body > 0:
+        ep[pl.ds(0, body), :] = e_s[pl.ds(0, body), :]
+    if vb > body:
+        ep[pl.ds(body, vb - body), :] = jnp.zeros((vb - body, d), BF16)
+        ep[pl.ds(body, real - body), :] = e_s[pl.ds(body, real - body), :]
+    e_pair = cube.pair(ep.at[pl.ds(0, vb)], ep.at[pl.ds(vb, vb)])
     e_pair.start()
     w_pair = [cube.pair(src.at[:, span(1 - c, half_f)], dst.at[mine_d]) for src, dst in ((wg, wgh), (wu, wuh))]
     cube.start(w_pair + w_local)
-    cube.finish([e_local, e_pair])
+    e_pair.wait()
     outs = [local(ep, ep_o), local(wgh, wgh_o), local(wuh, wuh_o)]
     outs[0].start()
     chunk = min(256, cube.rows)
 
     def lookup(i):
         at = span(i, chunk)
-        xnat[at, :] = tn(one_hot(2 * vb, idx[:, at]), ep[...]).astype(BF16)
+        xnat[at, :] = tn(one_hot(2 * vb, table_rows(cube, real, vb, ids[:, at])), ep[...]).astype(BF16)
 
     loop(0, cube.rows // chunk, lookup)
     cube.spread(xnat, xb)
@@ -335,8 +368,8 @@
 
 
 def head_kernel(
-    cube, vb, real, num_tokens, hn, ep, lab, h_own, g2, x_own, g1, gt_own, u_own, wgh_i, wuh_i, wd_i,
-    dmf, loss, deh, dx_own, at_o, gt_o, u_o, *scratch
+    cube, vb, real, num_tokens, hn, ep, labels, h_own, g2, x_own, g1, gt_own, u_own, wgh_i, wuh_i, wd_i,
+    dm_nat, loss, deh, dx_own, at_o, gt_o, u_o, *scratch
 ):
     z, dz, nat, stats, lbuf, dm32, mp, mr, wgh, wuh, wd, xf, tstage, stage, psend, precv, lsem, osem, st_s, st_r, *rest = scratch
     rb, rr, gb, xg = by(COLORS, rest[: 4 * COLORS])
@@ -362,7 +395,7 @@
         zz = jnp.where(valid, nt(ep[...], hn[at, :]), -1e38)
         z[:, at] = zz
         top = jnp.max(zz, axis=0, keepdims=True)
-        parts = {TOP: top, SUM: jnp.exp(zz - top), LABEL: jnp.where(row == lab[:, at], zz, 0.0)}
+        parts = {TOP: top, SUM: jnp.exp(zz - top), LABEL: jnp.where(row == table_rows(cube, real, vb, labels[:, at]), zz, 0.0)}
         for r, v in parts.items():
             stats[0, mine, pl.ds(r, 1), at] = v if r == TOP else jnp.sum(v, axis=0, keepdims=True)
 
@@ -375,10 +408,10 @@
         cube.finish(copies)
         if xstep > 1:
             xstep = cube.ag_next(xg, xg_sems, xstep)
-        tops, sums, labels = [[stats[a, i, pl.ds(r, 1), :] for i in range(RING)] for r in range(LABEL + 1)]
+        tops, sums, marks = [[stats[a, i, pl.ds(r, 1), :] for i in range(RING)] for r in range(LABEL + 1)]
         top = functools.reduce(jnp.maximum, tops)
         total = sum(v * jnp.exp(m - top) for m, v in zip(tops, sums))
-        label = sum(labels)
+        label = sum(marks)
         slot = cube.digits[a + 1] if a + 1 < cube.axes else 0
         for r, v in enumerate((top, total, label)):
             stats[a + 1, slot, pl.ds(r, 1), :] = v
@@ -394,7 +427,7 @@
         at = span(i, chunk)
         row = lax.broadcasted_iota(jnp.int32, (2 * vb, chunk), 0)
         soft = jnp.exp(z[:, at] - final[pl.ds(TOP, 1), at]) / final[pl.ds(SUM, 1), at]
-        dzz = (jnp.where(row == lab[:, at], soft - 1.0, soft) / num_tokens).astype(BF16)
+        dzz = (jnp.where(row == table_rows(cube, real, vb, labels[:, at]), soft - 1.0, soft) / num_tokens).astype(BF16)
         dz[:, at] = dzz
         nat[at, :] = tn(dzz, ep[...])
 
@@ -402,7 +435,6 @@
     cube.spread(nat, rb)
     mine_t = span(c, t)
     xf_pair = cube.pair(xf.at[mine_t], xf.at[mine_t])
-    dm_pair = cube.pair(dmf.at[mine_t], dmf.at[mine_t])
     d_pair = cube.pair(dm32.at[0], dm32.at[1])
     m_pair = cube.pair(mp.at[1], mr)
     t_out = local(tstage, at_o)
@@ -426,14 +458,13 @@
         loop(0, 2 * t // tile, body)
         cube.start(out_copies(p))
 
-    def normalise():
-        def body(i):
-            at = span(i, chunk)
-            val = rms_scale(xf[at, :].astype(F32), g1[...])
-            xf[at, :] = val.astype(BF16)
-            tstage[:, at] = val.T.astype(BF16)
-
-        loop(0, 2 * chunks, body)
+    def normalise(i):
+        at = span(c * chunks + i, chunk)
+        xf[at, :] = rms_scale(xf[at, :].astype(F32), g1[...]).astype(BF16)
+
+    def transpose(half, i):
+        at = span(half * chunks + i, chunk)
+        tstage[:, at] = xf[at, :].astype(F32).T.astype(BF16)
 
     def head_grad(i):
         deh[span(i, vb), :] = nn(dz[span(i, vb), :], hn[...])
@@ -447,16 +478,19 @@
 
     def rs_fill(s):
         if s == 0:
-            loop(0, 2, head_grad)
             cube.ag_next(xg, xg_sems, xstep)
             cube.collect(xg, xf, c)
+            loop(0, chunks, normalise)
             xf_pair.start()
+            loop(0, 2, head_grad)
+            loop(0, chunks, functools.partial(transpose, c))
+        elif s == 1:
             cube.finish(w_copies + [xf_pair])
-            normalise()
+            loop(0, chunks, functools.partial(transpose, 1 - c))
             t_out.start()
-            run(1)
+            run(2)
         else:
-            run(walk + 1 - s)
+            run(2)
 
     cube.reduce_scatter(rb, rr, rs_sems, rs_fill)
     dh = rms_back(h_own[...], g2[...], cube.get_own(rb))
@@ -487,26 +521,29 @@
 
     d_pair.start()
     cube.all_gather(gb, ag_sems, ag_fill)
-    cube.collect(gb, dmf, c)
-    dm_pair.start()
+    cube.collect(gb, dm_nat)
     run(PARTS)
     m_pair.wait()
     dx_own[...] = dh + rms_back(x_own[...].astype(F32), g1[...], mp[0] + mr[...])
     l_pair.wait()
-    loss[...] = (lbuf[0] + lbuf[1]) / num_tokens
+    loss[0, 0] = jnp.max((lbuf[0] + lbuf[1]) / num_tokens)
     t_out.wait()
-    cube.finish(out_copies(PARTS - 2) + out_copies(PARTS - 1) + [dm_pair])
-
-
-def table_kernel(cube, vb, idx, dx_own, dmf, wd, deh, at_i, gt_i, u_i, de, act_o, dg_o, du_o, got_g, got_u, *scratch):
-    nat, mix, de_r, aoth, fin, fout, part, psend, precv, lsem, isem, osem, gsend, grecv, *rest = scratch
+    cube.finish(out_copies(PARTS - 2) + out_copies(PARTS - 1))
+
+
+def table_kernel(cube, vb, real, ids, dx_own, dm_i, wd_i, deh, at_i, gt_i, u_i, de, dmf_o, act_o, dg_o, du_o, got_g, got_u, *scratch):
+    dmf, wd, nat, mix, de_r, aoth, fin, fout, part, psend, precv, lsem, isem, osem, gsend, grecv, *rest = scratch
     gb, ag_sems = rest[:COLORS], rest[COLORS:]
     cube.bind(psend, precv)
     c = cube.c
     t = cube.rows
     fc = wd.shape[0] // PARTS
     half_d = aoth.shape[0]
-    a_copy = pltpu.make_async_copy(at_i.at[span(1 - c, half_d)], aoth, lsem)
+    local = Local(lsem)
+    mine_t = span(c, t)
+    dm_copy, wd_copy, a_copy = local(dm_i, dmf.at[mine_t]), local(wd_i, wd), local(at_i.at[span(1 - c, half_d)], aoth)
+    deh_copy, dm_out = local(deh, mix), local(dmf, dmf_o)
+    dm_pair = cube.pair(dm_i, dmf.at[mine_t])
 
     def in_copies(p):
         return [pltpu.make_async_copy(src.at[p], fin.at[p % 2, i], isem.at[i, p]) for i, src in enumerate((gt_i, u_i))]
@@ -528,13 +565,14 @@
         for copy in send_copies(p):
             copy.wait_send()
 
-    cube.start([a_copy] + in_copies(0))
+    cube.start([dm_copy, wd_copy] + in_copies(0) + [a_copy, deh_copy])
     cube.put_own(gb, dx_own[...])
     cube.barrier()
     step = cube.ag_start(gb, ag_sems)
-    mix[...] = deh[...]
-    a_copy.wait()
-    tile = min(512, 2 * t)
+    dm_pair.start()
+    cube.finish([dm_copy, wd_copy, a_copy])
+    tile = min(512, t)
+    tiles = t // tile
     for p in range(PARTS):
         if p + 1 < PARTS:
             cube.start(in_copies(p + 1))
@@ -543,8 +581,8 @@
             drain(p - 2)
         src, dst, res = fin.at[p % 2], fout.at[p % 2], part.at[p % 2]
 
-        def body(i):
-            at = span(i, tile)
+        def body(half, i):
+            at = span(half * tiles + i, tile)
             d_act = nt(dmf[at, :], wd[pl.ds(p * fc, fc), :])
             gate = src[0, at, :].astype(F32)
             up = src[1, at, :].astype(F32)
@@ -554,20 +592,27 @@
             for which, v in enumerate(outs):
                 dst[which, at, :] = v.astype(BF16)
 
-        loop(0, 2 * t // tile, body)
+        if p == 0:
+            loop(0, tiles, functools.partial(body, c))
+            dm_pair.wait()
+            dm_out.start()
+            loop(0, tiles, functools.partial(body, 1 - c))
+        else:
+            loop(0, 2 * tiles, functools.partial(body, 0))
         for which in range(2):
             res[which] = nn(aoth[...], dst[which + 1])
         cube.start(out_copies(p) + send_copies(p))
-        if step > 0 and p % 2 < 1:
+        if step > 0 and p % 2 == 0:
             step = cube.ag_next(gb, ag_sems, step)
     while step >= 0:
         step = cube.ag_next(gb, ag_sems, step)
     cube.collect(gb, nat)
+    cube.finish([deh_copy, dm_out])
     chunk = min(256, t)
 
     def scatter(i):
         at = span(i, chunk)
-        hot = one_hot(2 * vb, idx[:, at])
+        hot = one_hot(2 * vb, table_rows(cube, real, vb, ids[:, at]))
         val = nat[at, :]
         hi = val.astype(BF16)
         rest = val - hi.astype(F32)
@@ -587,22 +632,81 @@
     de[...] = mix[pl.ds(0, vb), :] + de_r[...]
 
 
-def weight_kernel(core, aown, dg, du, act, dmf, got_g, got_u, og, ou, od):
-    even = pl.program_id(0) % 2 == 0
-    n, _, fc = dg.shape
-
-    @pl.when(even)
-    def _():
-        for i in range(n):
-            og[:, pl.ds(i * fc, fc)] = nn(aown[...], dg[i])
-            ou[:, pl.ds(i * fc, fc)] = nn(aown[...], du[i])
-
-    @pl.when(jnp.logical_not(even))
-    def _():
-        for i in range(n):
-            og[:, pl.ds(i * fc, fc)] = got_g[i]
-            ou[:, pl.ds(i * fc, fc)] = got_u[i]
-            od[pl.ds(i * fc, fc), :] = tn(act[i], dmf[...])
+def weight_kernel(loss, de, at_i, dg, du, act, dmf_i, got_g, got_u, loss_o, de_o, og, ou, od, *scratch):
+    aown, dmf, ring, gring, ostage, dstage, de_s, de_t, lsem, rsem, gsem, osem, xsem = scratch
+    c = lax.axis_index("fsdp")
+    depth, fc = ring.shape[0], ring.shape[-1]
+    parts, half_f = dg.shape[0], dg.shape[0] * fc
+    local = Local(lsem)
+    a_copy, dm_copy = local(at_i.at[span(c, aown.shape[0])], aown), local(dmf_i, dmf)
+    de_in, de_out = local(de, de_s), local(de_t, de_o)
+
+    def reads(p):
+        slot = lax.rem(p, depth)
+        grads = [pltpu.make_async_copy(src.at[p], ring.at[slot, i], rsem.at[i, slot]) for i, src in enumerate((dg, du, act))]
+        return grads, [pltpu.make_async_copy(src.at[p], gring.at[slot, i], gsem.at[i, slot]) for i, src in enumerate((got_g, got_u))]
+
+    def columns(half, p):
+        return pl.ds(pl.multiple_of(half * half_f + p * fc, fc), fc)
+
+    def passes(p):
+        slot = lax.rem(p, depth)
+        return [pltpu.make_async_copy(gring.at[slot, i], dst.at[:, columns(1 - c, p)], xsem.at[i, slot]) for i, dst in enumerate((og, ou))]
+
+    def writes(p):
+        slot = lax.rem(p, 2)
+        out = [pltpu.make_async_copy(ostage.at[slot, i], dst.at[:, columns(c, p)], osem.at[i, slot]) for i, dst in enumerate((og, ou))]
+        return out + [pltpu.make_async_copy(dstage.at[slot], od.at[span(p, fc)], osem.at[2, slot])]
+
+    def each(copies, verb):
+        for copy in copies:
+            getattr(copy, verb)()
+
+    def fetch(p):
+        grads, got = reads(p)
+        each(grads + got, "start")
+
+    a_copy.start()
+    fetch(0)
+    dm_copy.start()
+    for p in range(1, depth):
+        fetch(p)
+    de_in.start()
+    a_copy.wait()
+    loss_o[0, 0] = loss[0, 0]
+
+    def body(p):
+        slot, oslot = lax.rem(p, depth), lax.rem(p, 2)
+        grads, got = reads(p)
+        each(got, "wait")
+        each(passes(p), "start")
+        each(grads, "wait")
+
+        @pl.when(p >= 2)
+        def _():
+            each(writes(p - 2), "wait")
+
+        for i in range(2):
+            ostage[oslot, i] = nn(aown[...], ring[slot, i])
+
+        @pl.when(p == 0)
+        def _():
+            dm_copy.wait()
+
+        dstage[oslot] = tn(ring[slot, 2], dmf[...])
+        each(writes(p), "start")
+        each(passes(p), "wait")
+
+        @pl.when(p + depth < parts)
+        def _():
+            fetch(p + depth)
+
+    loop(0, parts, body)
+    de_in.wait()
+    de_t[...] = de_s[pl.ds(0, de_t.shape[0]), :]
+    de_out.start()
+    each(writes(parts - 2) + writes(parts - 1), "wait")
+    de_out.wait()
 
 
 def solution(mesh):
@@ -628,18 +732,8 @@
         fc = half_f // PARTS
         cube = Cube(model, t, d)
         last = cube.last
-        me, core = lax.axis_index("model"), lax.axis_index("fsdp")
-        first = (2 * me + core) * real
-        other = (2 * me + 1 - core) * real
-
-        def local_rows(ids):
-            flat = ids.reshape(1, t)
-            here, there = flat - first, flat - other
-            return jnp.where((here >= 0) & (here < real), here, jnp.where((there >= 0) & (there < real), vb + there, -1))
-
-        idx = local_rows(tok_ids)
-        lab = local_rows(tok_labels)
-        table = jnp.pad(table_shard, ((0, vb - real), (0, 0)))
+        ids, labels = tok_ids.reshape(1, t), tok_labels.reshape(1, t)
+        smem = pl.BlockSpec(memory_space=pltpu.SMEM)
         g1, g2 = gain_in.reshape(1, d), gain_out.reshape(1, d)
         act_own = sds((2 * last, half_f), BF16)
         w_half = sds((d, half_f), BF16)
@@ -649,6 +743,7 @@
             in_specs=[vmem, hbm, hbm, hbm, hbm, vmem, vmem],
             out_specs=(vmem, hbm, hbm, hbm, vmem, vmem, vmem, vmem),
             scratch_shapes=[
+                pltpu.VMEM((real, d), BF16),
                 pltpu.VMEM((half_f, d), BF16),
                 pltpu.VMEM((2 * vb, d), BF16),
                 pltpu.VMEM((d, half_f), BF16),
@@ -665,13 +760,13 @@
             + cube.sems(2),
             compiler_params=params(0),
             name="embed",
-        )(idx, table, gate_shard, up_shard, down_shard, g1, g2)
+        )(ids, table_shard, gate_shard, up_shard, down_shard, g1, g2)
         chunked = sds((PARTS, 2 * t, fc), BF16)
-        dmf, loss, deh, dx_own, a_t, gt, u = pl.pallas_call(
+        dm, loss, deh, dx_own, a_t, gt, u = pl.pallas_call(
             functools.partial(head_kernel, cube, vb, real, num_tokens),
-            out_shape=(sds((2 * t, d), BF16), sds((8, 128), F32), sds((2 * vb, d), F32), sds((last, d), F32), sds((d, 2 * t), BF16), chunked, chunked),
+            out_shape=(sds((t, d), BF16), sds((1, 1), F32), sds((2 * vb, d), F32), sds((last, d), F32), sds((d, 2 * t), BF16), chunked, chunked),
             in_specs=[vmem] * 9 + [hbm] * 3,
-            out_specs=(vmem,) * 4 + (hbm,) * 3,
+            out_specs=(vmem, smem, vmem, vmem) + (hbm,) * 3,
             scratch_shapes=[
                 pltpu.VMEM((2 * vb, t), F32),
                 pltpu.VMEM((2 * vb, t), BF16),
@@ -698,14 +793,16 @@
             + cube.sems(3),
             compiler_params=params(1),
             name="head",
-        )(hn, ep, lab, h_own, g2, x_own, g1, gt_own, u_own, wgh, wuh, down_shard)
+        )(hn, ep, labels, h_own, g2, x_own, g1, gt_own, u_own, wgh, wuh, down_shard)
         got = sds((PARTS, half_d, fc), F32)
-        de, act, d_gate, d_up, got_g, got_u = pl.pallas_call(
-            functools.partial(table_kernel, cube, vb),
-            out_shape=(sds((vb, d), F32), chunked, chunked, chunked, got, got),
-            in_specs=[vmem] * 5 + [hbm] * 3,
-            out_specs=(vmem,) + (hbm,) * 5,
+        de, dmf, act, d_gate, d_up, got_g, got_u = pl.pallas_call(
+            functools.partial(table_kernel, cube, vb, real),
+            out_shape=(sds((vb, d), F32), sds((2 * t, d), BF16), chunked, chunked, chunked, got, got),
+            in_specs=[vmem] * 2 + [hbm] * 6,
+            out_specs=(vmem,) + (hbm,) * 6,
             scratch_shapes=[
+                pltpu.VMEM((2 * t, d), BF16),
+                pltpu.VMEM((half_f, d), BF16),
                 pltpu.VMEM((t, d), F32),
                 pltpu.VMEM((2 * vb, d), F32),
                 pltpu.VMEM((vb, d), F32),
@@ -713,9 +810,9 @@
                 pltpu.VMEM((2, 2, 2 * t, fc), BF16),
                 pltpu.VMEM((2, 3, 2 * t, fc), BF16),
                 pltpu.VMEM((2, 2, half_d, fc), F32),
-                dma((1,)),
-                dma((1,)),
-                dma,
+                dma((2,)),
+                dma((2,)),
+                dma((5,)),
                 dma((2, PARTS)),
                 dma((3, PARTS)),
                 dma((2, PARTS)),
@@ -725,31 +822,31 @@
             + cube.sems(1),
             compiler_params=params(2),
             name="table",
-        )(idx, dx_own, dmf, down_shard, deh, a_t, gt, u)
-        wide = 2
-        chunk_spec = pl.BlockSpec((wide, 2 * t, fc), lambda i, s: (i // 2, 0, 0))
-        got_spec = pl.BlockSpec((wide, half_d, fc), lambda i, s: (i // 2, 0, 0))
-        grad_spec = pl.BlockSpec((half_d, wide * fc), lambda i, s: (0, (s[0] + i % 2) % 2 * (PARTS // wide) + i // 2))
-        grad_gate, grad_up, grad_down = pl.pallas_call(
+        )(ids, dx_own, dm, down_shard, deh, a_t, gt, u)
+        depth = 3
+        loss, de, grad_gate, grad_up, grad_down = pl.pallas_call(
             weight_kernel,
-            out_shape=(sds((half_d, f), F32), sds((half_d, f), F32), sds((half_f, d), F32)),
-            grid_spec=pltpu.PrefetchScalarGridSpec(
-                num_scalar_prefetch=1,
-                grid=(2 * PARTS // wide,),
-                in_specs=[
-                    pl.BlockSpec((half_d, 2 * t), lambda i, s: (s[0], 0)),
-                    chunk_spec,
-                    chunk_spec,
-                    chunk_spec,
-                    pl.BlockSpec((2 * t, d), lambda i, s: (0, 0)),
-                    got_spec,
-                    got_spec,
-                ],
-                out_specs=(grad_spec, grad_spec, pl.BlockSpec((wide * fc, d), lambda i, s: (i // 2, 0))),
-            ),
-            compiler_params=pltpu.CompilerParams(vmem_limit_bytes=VMEM_LIMIT),
+            out_shape=(sds((1, 1), F32), sds((real, d), F32), sds((half_d, f), F32), sds((half_d, f), F32), sds((half_f, d), F32)),
+            in_specs=[smem] + [hbm] * 8,
+            out_specs=(smem,) + (hbm,) * 4,
+            scratch_shapes=[
+                pltpu.VMEM((half_d, 2 * t), BF16),
+                pltpu.VMEM((2 * t, d), BF16),
+                pltpu.VMEM((depth, 3, 2 * t, fc), BF16),
+                pltpu.VMEM((depth, 2, half_d, fc), F32),
+                pltpu.VMEM((2, 2, half_d, fc), F32),
+                pltpu.VMEM((2, fc, d), F32),
+                pltpu.VMEM((vb, d), F32),
+                pltpu.VMEM((real, d), F32),
+                dma((4,)),
+                dma((3, depth)),
+                dma((2, depth)),
+                dma((3, 2)),
+                dma((2, depth)),
+            ],
+            compiler_params=pltpu.CompilerParams(vmem_limit_bytes=VMEM_LIMIT, has_side_effects=True),
             name="weights",
-        )(core.reshape(1).astype(jnp.int32), a_t, d_gate, d_up, act, dmf, got_g, got_u)
-        return loss[0, 0], de[:real], grad_gate, grad_up, grad_down
+        )(loss, de, a_t, d_gate, d_up, act, dmf, got_g, got_u)
+        return loss.reshape(()), de, grad_gate, grad_up, grad_down
 
     return jax.shard_map(device_step, mesh=mesh, in_specs=(tok_spec, tok_spec, row_spec, weight_spec, weight_spec, weight_spec, P(), P()), out_specs=(P(), row_spec, weight_spec, weight_spec, weight_spec), check_vma=False)

time: 256 us -> 219 us (0.86)
  Pallas kernels: 248 us -> 218 us
  local copies, waits for them, and re-layouts: 6.06 us -> 0 us
    pallas_call x1, Pallas kernels: 97.1 us -> 85 us  [device_step(): pl.pallas_call(functools.partial(head_kernel, cube, vb, real, num_tokens)...]
    pallas_call x2, Pallas kernels: 88.7 us -> 77.1 us  [the longest x1 48.9 us: device_step(): pl.pallas_call(functools.partial(table_kernel, cube, vb, real), out_shape...]
    pallas_call x1, Pallas kernels: 61.9 us -> 55.8 us  [device_step(): pl.pallas_call(functools.partial(embed_kernel, cube, vb), out_shape=(sds(...]
    unnamed x1 -> x0, local copies, waits for them, and re-layouts: 2.78 us -> none
where the time goes in v2:
time: 219 us
  Pallas kernels  218 us (100%)
    pallas_call x1, Pallas kernels, device_step(): pl.pallas_call(functools.partial(head_kernel, cube, vb, real, num_tokens)...  85 us
    pallas_call x1, Pallas kernels, device_step(): pl.pallas_call(functools.partial(embed_kernel, cube, vb), out_shape=(sds(...  55.8 us
    pallas_call x1, Pallas kernels, device_step(): pl.pallas_call(functools.partial(table_kernel, cube, vb, real), out_shape...  48.9 us
    pallas_call x1, Pallas kernels, device_step(): pl.pallas_call(weight_kernel, out_shape=(sds((1, 1), F32), sds((real, d),...  28.1 us

profile of v2, /device:TPU:1, one launch (start us, length us, event | category | flops | bytes accessed | tf_op | source)
XLA Modules:
  0.0 218.7 jit_solution(14213680459390401663)
XLA Ops:
  0.6 55.8 %embed.1 = (bf16[1024,1024]{1,0:T(8,128)(2,1)}, bf16[800,1024]{1,0:T(8,128)(2,1)}, bf16[1024,2048]{1,0:T(8,128)(2,1)}, bf16[1024,2048]{1,0:T(8,128)(2,1)}, f32[1...) custom-call(s32[1,1024]{1,0:T(1,128)} %ids.3, ...), custom_call_target="tpu_custom_call" | custom-call | tf_op jit(solution)/shard_map/embed/pallas_call | solution.py:740
  56.4 85.0 %head.1 = (bf16[1024,1024]{1,0:T(8,128)(2,1)}, f32[1,1]{1,0:T(1,128)}, f32[800,1024]{1,0:T(8,128)}, f32[16,1024]{1,0:T(8,128)}, bf16[1024,2048]{1,0:T(8,128)(2,1...) custom-call(bf16[1024,1024]{1,0:T(8,128)(2,1)} %get-tuple-element.32.hn, ...), custom_call_target="tpu_custom_call" | custom-call | tf_op jit(solution)/shard_map/head/pallas_call | solution.py:765
  141.5 48.9 %table.1 = (f32[400,1024]{1,0:T(8,128)}, bf16[2048,1024]{1,0:T(8,128)(2,1)}, bf16[8,2048,256]{2,1,0:T(8,128)(2,1)}, bf16[8,2048,256]{2,1,0:T(8,128)(2,1)}, bf16[...) custom-call(s32[1,1024]{1,0:T(1,128)} %ids.3, f32[16,1024]{1,0:T(8,128)} %get-tuple-element.41.dx_own, ...), custom_call_target="tpu_custom_call" | custom-call | tf_op jit(solution)/shard_map/table/pallas_call | solution.py:798
  190.4 28.1 %weights.1 = (f32[1,1]{1,0:T(1,128)}, f32[393,1024]{1,0:T(8,128)}, f32[512,4096]{1,0:T(8,128)}, f32[512,4096]{1,0:T(8,128)}, f32[2048,1024]{1,0:T(8,128)}) custom-call(f32[1,1]{1,0:T(1,128)} %get-tuple-element.40.loss, f32[400,1024]{1,0:T(8,128)} %get-tuple-element.47.de, bf16[1024,2048]{1,0:T(8,128)(2,1)} %get-tuple-element.44.at_i, ...), custom_call_target="tpu_custom_call" | custom-call | tf_op jit(solution)/shard_map/weights/pallas_call | solution.py:827

commit v3 on v2

--- a/solution.py
+++ b/solution.py
@@ -131,8 +131,7 @@
         b = self.digits[a]
         return self.m + RING**a * ((b + step) % RING - b)
 
-    def barrier(self, rings=False):
-        sem = pltpu.get_barrier_semaphore()
+    def arrive(self, rings=False):
         peers = [(self.m, 1 - self.c)]
         for k in range(COLORS):
             steps = [[s] for s in range(self.walk)] + [self.group(q + 1) for q in range(self.peers)]
@@ -140,8 +139,11 @@
         if rings:
             peers += [(self.ring_peer(a, step), self.c) for a in range(self.axes) for step in range(1, RING)]
         for peer in peers:
-            pl.semaphore_signal(sem, inc=1, device_id=peer, device_id_type=MESH)
-        pl.semaphore_wait(sem, len(peers))
+            pl.semaphore_signal(pltpu.get_barrier_semaphore(), inc=1, device_id=peer, device_id_type=MESH)
+        self.expected = len(peers)
+
+    def meet(self):
+        pl.semaphore_wait(pltpu.get_barrier_semaphore(), self.expected)
 
     def place(self, k, j):
         pos = []
@@ -301,6 +303,7 @@
     xb, xr, hb = by(COLORS, rest[: 3 * COLORS])
     rs_sems, hg_sems = by(2, rest[3 * COLORS :])
     cube.bind(psend, precv)
+    cube.arrive()
     local = Local(lsem)
     c = cube.c
     d = hn.shape[1]
@@ -310,7 +313,6 @@
     e_local = local(e_ref, e_s)
     e_local.start()
     w_local = [local(wd, wd_s), local(wg.at[:, span(c, half_f)], wgh.at[mine_d]), local(wu.at[:, span(c, half_f)], wuh.at[mine_d])]
-    cube.barrier()
     e_local.wait()
     real = e_s.shape[0]
     body = real - real % 16
@@ -319,20 +321,27 @@
     if vb > body:
         ep[pl.ds(body, vb - body), :] = jnp.zeros((vb - body, d), BF16)
         ep[pl.ds(body, real - body), :] = e_s[pl.ds(body, real - body), :]
+    cube.meet()
     e_pair = cube.pair(ep.at[pl.ds(0, vb)], ep.at[pl.ds(vb, vb)])
     e_pair.start()
     w_pair = [cube.pair(src.at[:, span(1 - c, half_f)], dst.at[mine_d]) for src, dst in ((wg, wgh), (wu, wuh))]
     cube.start(w_pair + w_local)
+    chunk = min(256, cube.rows)
+
+    def lookup(i):
+        at = span(i, chunk)
+        xnat[at, :] = tn(one_hot(vb, table_rows(cube, real, vb, ids[:, at])), ep[pl.ds(0, vb), :]).astype(BF16)
+
+    def lookup_other(i):
+        at = span(i, chunk)
+        found = tn(one_hot(vb, table_rows(cube, real, vb, ids[:, at]) - vb), ep[pl.ds(vb, vb), :])
+        xnat[at, :] = (xnat[at, :].astype(F32) + found).astype(BF16)
+
+    loop(0, cube.rows // chunk, lookup)
     e_pair.wait()
     outs = [local(ep, ep_o), local(wgh, wgh_o), local(wuh, wuh_o)]
     outs[0].start()
-    chunk = min(256, cube.rows)
-
-    def lookup(i):
-        at = span(i, chunk)
-        xnat[at, :] = tn(one_hot(2 * vb, table_rows(cube, real, vb, ids[:, at])), ep[...]).astype(BF16)
-
-    loop(0, cube.rows // chunk, lookup)
+    loop(0, cube.rows // chunk, lookup_other)
     cube.spread(xnat, xb)
     cube.reduce_scatter(xb, xr, rs_sems)
     x_own[...] = cube.get_own(xb)
@@ -368,22 +377,23 @@
 
 
 def head_kernel(
-    cube, vb, real, num_tokens, hn, ep, labels, h_own, g2, x_own, g1, gt_own, u_own, wgh_i, wuh_i, wd_i,
-    dm_nat, loss, deh, dx_own, at_o, gt_o, u_o, *scratch
+    cube, vb, real, num_tokens, hn_i, ep_i, labels, h_own, g2, x_own, g1, gt_own, u_own, wgh_i, wuh_i, wd_i,
+    dm_nat, loss, deh_o, dx_own, at_o, gt_o, u_o, *scratch
 ):
-    z, dz, nat, stats, lbuf, dm32, mp, mr, wgh, wuh, wd, xf, tstage, stage, psend, precv, lsem, osem, st_s, st_r, *rest = scratch
+    hn, ep, z, dz, nat, stats, lbuf, dm32, mp, mr, wgh, wuh, wd, xf, tstage, stage, psend, precv, lsem, osem, st_s, st_r, *rest = scratch
     rb, rr, gb, xg = by(COLORS, rest[: 4 * COLORS])
     rs_sems, ag_sems, xg_sems = by(2, rest[4 * COLORS :])
     cube.bind(psend, precv)
+    cube.arrive(rings=True)
     local = Local(lsem)
     c = cube.c
     t, d = hn.shape
     walk, last = cube.walk, cube.last
+    first = [local(ep_i, ep), local(hn_i, hn)]
+    cube.start(first)
     w_copies = [local(wgh_i, wgh), local(wuh_i, wuh), local(wd_i, wd)]
     cube.start(w_copies)
     cube.put_own(xg, x_own[...])
-    cube.barrier(rings=True)
-    xstep = cube.ag_start(xg, xg_sems)
     chunk = min(256, t)
     chunks = t // chunk
     mine = cube.digits[0]
@@ -399,7 +409,11 @@
         for r, v in parts.items():
             stats[0, mine, pl.ds(r, 1), at] = v if r == TOP else jnp.sum(v, axis=0, keepdims=True)
 
-    loop(0, chunks, logits)
+    cube.finish(first)
+    loop(0, chunks // 2, logits)
+    cube.meet()
+    xstep = cube.ag_start(xg, xg_sems)
+    loop(chunks // 2, chunks, logits)
     xstep = cube.ag_next(xg, xg_sems, xstep)
     for a in range(cube.axes):
         here = stats.at[a, cube.digits[a]]
@@ -422,6 +436,8 @@
     l_pair = cube.pair(lbuf.at[c], lbuf.at[c])
     l_pair.start()
     final = stats.at[cube.axes, 0]
+    deh = z.at[:, pl.ds(0, d)]
+    deh_out = local(deh, deh_o)
 
     def backward(i):
         at = span(i, chunk)
@@ -483,6 +499,7 @@
             loop(0, chunks, normalise)
             xf_pair.start()
             loop(0, 2, head_grad)
+            deh_out.start()
             loop(0, chunks, functools.partial(transpose, c))
         elif s == 1:
             cube.finish(w_copies + [xf_pair])
@@ -527,7 +544,7 @@
     dx_own[...] = dh + rms_back(x_own[...].astype(F32), g1[...], mp[0] + mr[...])
     l_pair.wait()
     loss[0, 0] = jnp.max((lbuf[0] + lbuf[1]) / num_tokens)
-    t_out.wait()
+    cube.finish([t_out, deh_out])
     cube.finish(out_copies(PARTS - 2) + out_copies(PARTS - 1))
 
 
@@ -535,6 +552,7 @@
     dmf, wd, nat, mix, de_r, aoth, fin, fout, part, psend, precv, lsem, isem, osem, gsend, grecv, *rest = scratch
     gb, ag_sems = rest[:COLORS], rest[COLORS:]
     cube.bind(psend, precv)
+    cube.arrive()
     c = cube.c
     t = cube.rows
     fc = wd.shape[0] // PARTS
@@ -567,7 +585,7 @@
 
     cube.start([dm_copy, wd_copy] + in_copies(0) + [a_copy, deh_copy])
     cube.put_own(gb, dx_own[...])
-    cube.barrier()
+    cube.meet()
     step = cube.ag_start(gb, ag_sems)
     dm_pair.start()
     cube.finish([dm_copy, wd_copy, a_copy])
@@ -610,19 +628,21 @@
     cube.finish([deh_copy, dm_out])
     chunk = min(256, t)
 
-    def scatter(i):
+    def scatter(half, i):
         at = span(i, chunk)
-        hot = one_hot(2 * vb, table_rows(cube, real, vb, ids[:, at]))
+        rows = pl.ds(half * vb, vb)
+        hot = one_hot(vb, table_rows(cube, real, vb, ids[:, at]) - half * vb)
         val = nat[at, :]
         hi = val.astype(BF16)
         rest = val - hi.astype(F32)
         mid = rest.astype(BF16)
         low = (rest - mid.astype(F32)).astype(BF16)
-        mix[...] = mix[...] + ((nn(hot, low) + nn(hot, mid)) + nn(hot, hi))
-
-    loop(0, t // chunk, scatter)
+        mix[rows, :] = mix[rows, :] + ((nn(hot, low) + nn(hot, mid)) + nn(hot, hi))
+
+    loop(0, t // chunk, functools.partial(scatter, 1))
     e_pair = cube.pair(mix.at[pl.ds(vb, vb)], de_r)
     e_pair.start()
+    loop(0, t // chunk, functools.partial(scatter, 0))
     drain(PARTS - 2)
     drain(PARTS - 1)
     for p in range(PARTS):
@@ -695,17 +715,20 @@
 
         dstage[oslot] = tn(ring[slot, 2], dmf[...])
         each(writes(p), "start")
-        each(passes(p), "wait")
-
-        @pl.when(p + depth < parts)
+
+        @pl.when(p >= 1)
         def _():
-            fetch(p + depth)
+            each(passes(p - 1), "wait")
+
+        @pl.when((p >= 1) & (p - 1 + depth < parts))
+        def _():
+            fetch(p - 1 + depth)
 
     loop(0, parts, body)
     de_in.wait()
     de_t[...] = de_s[pl.ds(0, de_t.shape[0]), :]
     de_out.start()
-    each(writes(parts - 2) + writes(parts - 1), "wait")
+    each(passes(parts - 1) + writes(parts - 2) + writes(parts - 1), "wait")
     de_out.wait()
 
 
@@ -765,10 +788,12 @@
         dm, loss, deh, dx_own, a_t, gt, u = pl.pallas_call(
             functools.partial(head_kernel, cube, vb, real, num_tokens),
             out_shape=(sds((t, d), BF16), sds((1, 1), F32), sds((2 * vb, d), F32), sds((last, d), F32), sds((d, 2 * t), BF16), chunked, chunked),
-            in_specs=[vmem] * 9 + [hbm] * 3,
-            out_specs=(vmem, smem, vmem, vmem) + (hbm,) * 3,
+            in_specs=[hbm] * 2 + [vmem] * 7 + [hbm] * 3,
+            out_specs=(vmem, smem, hbm, vmem) + (hbm,) * 3,
             scratch_shapes=[
-                pltpu.VMEM((2 * vb, t), F32),
+                pltpu.VMEM((t, d), BF16),
+                pltpu.VMEM((2 * vb, d), BF16),
+                pltpu.VMEM((2 * vb, max(t, d)), F32),
                 pltpu.VMEM((2 * vb, t), BF16),
                 pltpu.VMEM((t, d), F32),
                 pltpu.VMEM((cube.axes + 1, RING, RING, t), F32),
@@ -823,7 +848,7 @@
             compiler_params=params(2),
             name="table",
         )(ids, dx_own, dm, down_shard, deh, a_t, gt, u)
-        depth = 3
+        depth = 4
         loss, de, grad_gate, grad_up, grad_down = pl.pallas_call(
             weight_kernel,
             out_shape=(sds((1, 1), F32), sds((real, d), F32), sds((half_d, f), F32), sds((half_d, f), F32), sds((half_f, d), F32)),

time: 219 us -> 214 us (0.977)
  Pallas kernels: 218 us -> 213 us
    pallas_call x1, Pallas kernels: 85 us -> 82.7 us  [device_step(): pl.pallas_call(functools.partial(head_kernel, cube, vb, real, num_tokens)...]
    pallas_call x1, Pallas kernels: 48.9 us -> 46.6 us  [device_step(): pl.pallas_call(functools.partial(table_kernel, cube, vb, real), out_shape...]
where the time goes in v3:
time: 214 us
  Pallas kernels  213 us (100%)
    pallas_call x1, Pallas kernels, device_step(): pl.pallas_call(functools.partial(head_kernel, cube, vb, real, num_tokens)...  82.7 us
    pallas_call x1, Pallas kernels, device_step(): pl.pallas_call(functools.partial(embed_kernel, cube, vb), out_shape=(sds(...  54.6 us
    pallas_call x1, Pallas kernels, device_step(): pl.pallas_call(functools.partial(table_kernel, cube, vb, real), out_shape...  46.6 us
    pallas_call x1, Pallas kernels, device_step(): pl.pallas_call(weight_kernel, out_shape=(sds((1, 1), F32), sds((real, d),...  29.4 us

profile of v3, /device:TPU:1, one launch (start us, length us, event | category | flops | bytes accessed | tf_op | source)
XLA Modules:
  0.0 214.1 jit_solution(94986211334591755)
XLA Ops:
  0.6 54.6 %embed.1 = (bf16[1024,1024]{1,0:T(8,128)(2,1)}, bf16[800,1024]{1,0:T(8,128)(2,1)}, bf16[1024,2048]{1,0:T(8,128)(2,1)}, bf16[1024,2048]{1,0:T(8,128)(2,1)}, f32[1...) custom-call(s32[1,1024]{1,0:T(1,128)} %ids.3, ...), custom_call_target="tpu_custom_call" | custom-call | tf_op jit(solution)/shard_map/embed/pallas_call | solution.py:763
  55.2 82.7 %head.1 = (bf16[1024,1024]{1,0:T(8,128)(2,1)}, f32[1,1]{1,0:T(1,128)}, f32[800,1024]{1,0:T(8,128)}, f32[16,1024]{1,0:T(8,128)}, bf16[1024,2048]{1,0:T(8,128)(2,1...) custom-call(bf16[1024,1024]{1,0:T(8,128)(2,1)} %get-tuple-element.32.hn_i, ...), custom_call_target="tpu_custom_call" | custom-call | tf_op jit(solution)/shard_map/head/pallas_call | solution.py:788
  137.9 46.6 %table.1 = (f32[400,1024]{1,0:T(8,128)}, bf16[2048,1024]{1,0:T(8,128)(2,1)}, bf16[8,2048,256]{2,1,0:T(8,128)(2,1)}, bf16[8,2048,256]{2,1,0:T(8,128)(2,1)}, bf16[...) custom-call(s32[1,1024]{1,0:T(1,128)} %ids.3, f32[16,1024]{1,0:T(8,128)} %get-tuple-element.41.dx_own, ...), custom_call_target="tpu_custom_call" | custom-call | tf_op jit(solution)/shard_map/table/pallas_call | solution.py:823
  184.6 29.4 %weights.1 = (f32[1,1]{1,0:T(1,128)}, f32[393,1024]{1,0:T(8,128)}, f32[512,4096]{1,0:T(8,128)}, f32[512,4096]{1,0:T(8,128)}, f32[2048,1024]{1,0:T(8,128)}) custom-call(f32[1,1]{1,0:T(1,128)} %get-tuple-element.40.loss, f32[400,1024]{1,0:T(8,128)} %get-tuple-element.47.de, bf16[1024,2048]{1,0:T(8,128)(2,1)} %get-tuple-element.44.at_i, ...), custom_call_target="tpu_custom_call" | custom-call | tf_op jit(solution)/shard_map/weights/pallas_call | solution.py:852

commit v4 on v3

--- a/solution.py
+++ b/solution.py
@@ -326,7 +326,7 @@
     e_pair.start()
     w_pair = [cube.pair(src.at[:, span(1 - c, half_f)], dst.at[mine_d]) for src, dst in ((wg, wgh), (wu, wuh))]
     cube.start(w_pair + w_local)
-    chunk = min(256, cube.rows)
+    chunk = min(512, cube.rows)
 
     def lookup(i):
         at = span(i, chunk)
@@ -439,15 +439,17 @@
     deh = z.at[:, pl.ds(0, d)]
     deh_out = local(deh, deh_o)
 
+    wide = min(512, t)
+
     def backward(i):
-        at = span(i, chunk)
-        row = lax.broadcasted_iota(jnp.int32, (2 * vb, chunk), 0)
+        at = span(i, wide)
+        row = lax.broadcasted_iota(jnp.int32, (2 * vb, wide), 0)
         soft = jnp.exp(z[:, at] - final[pl.ds(TOP, 1), at]) / final[pl.ds(SUM, 1), at]
         dzz = (jnp.where(row == table_rows(cube, real, vb, labels[:, at]), soft - 1.0, soft) / num_tokens).astype(BF16)
         dz[:, at] = dzz
         nat[at, :] = tn(dzz, ep[...])
 
-    loop(0, chunks, backward)
+    loop(0, t // wide, backward)
     cube.spread(nat, rb)
     mine_t = span(c, t)
     xf_pair = cube.pair(xf.at[mine_t], xf.at[mine_t])
@@ -455,23 +457,25 @@
     m_pair = cube.pair(mp.at[1], mr)
     t_out = local(tstage, at_o)
     fc = wgh.shape[1] // PARTS
-    tile = min(512, 2 * t)
 
     def out_copies(p):
-        return [pltpu.make_async_copy(stage.at[p % 2, i], dst.at[p], osem.at[i, p]) for i, dst in enumerate((gt_o, u_o))]
+        slot = lax.rem(p, 2)
+        return [pltpu.make_async_copy(stage.at[slot, i], dst.at[p], osem.at[i, slot]) for i, dst in enumerate((gt_o, u_o))]
 
     def gate_up(p):
-        if p >= 2:
+        @pl.when(p >= 2)
+        def _():
             cube.finish(out_copies(p - 2))
-        cols = pl.ds(p * fc, fc)
-        slot = stage.at[p % 2]
+
+        cols = span(p, fc)
+        slot = stage.at[lax.rem(p, 2)]
 
         def body(i):
-            at = span(i, tile)
+            at = span(i, t)
             for which, w in enumerate((wgh, wuh)):
                 slot[which, at, :] = nn(xf[at, :], w[:, cols]).astype(BF16)
 
-        loop(0, 2 * t // tile, body)
+        loop(0, 2, body)
         cube.start(out_copies(p))
 
     def normalise(i):
@@ -485,12 +489,13 @@
     def head_grad(i):
         deh[span(i, vb), :] = nn(dz[span(i, vb), :], hn[...])
 
-    todo = list(range(PARTS))
+    todo = [0]
 
     def run(n):
-        while n > 0 and todo:
-            gate_up(todo.pop(0))
-            n -= 1
+        lo, hi = todo[0], min(todo[0] + n, PARTS)
+        todo[0] = hi
+        if lo < hi:
+            loop(lo, hi, gate_up)
 
     def rs_fill(s):
         if s == 0:
@@ -515,11 +520,10 @@
     cube.put_own(gb, dm)
     dm32[0] = dm
 
-    def token_back():
-        d_pair.wait()
+    def token_back(lo, hi):
         w = wgh.shape[1] // RING
         part = jnp.zeros((2 * last, d), F32)
-        for p in range(RING):
+        for p in range(lo, hi):
             at = pl.ds(p * w, w)
             d_act = nt(dm32[...].reshape(2 * last, d), wd[at, :])
             gate = gt_own[:, at].astype(F32)
@@ -527,12 +531,16 @@
             d_gate = (d_act * u_own[:, at].astype(F32) * (sig * (1.0 + gate * (1.0 - sig)))).astype(BF16)
             d_up = (d_act * (gate * sig)).astype(BF16)
             part = part + (nt(d_gate, wgh[:, at]) + nt(d_up, wuh[:, at]))
-        mp[...] = part.reshape(mp.shape)
-        m_pair.start()
+        part = part.reshape(mp.shape)
+        mp[...] = part if lo == 0 else mp[...] + part
 
     def ag_fill(s):
         if s == walk:
-            token_back()
+            d_pair.wait()
+            token_back(0, 2)
+        elif s == walk - 1:
+            token_back(2, RING)
+            m_pair.start()
         else:
             run(1)
 
@@ -545,7 +553,8 @@
     l_pair.wait()
     loss[0, 0] = jnp.max((lbuf[0] + lbuf[1]) / num_tokens)
     cube.finish([t_out, deh_out])
-    cube.finish(out_copies(PARTS - 2) + out_copies(PARTS - 1))
+    for p in (PARTS - 2, PARTS - 1):
+        cube.finish(out_copies(p))
 
 
 def table_kernel(cube, vb, real, ids, dx_own, dm_i, wd_i, deh, at_i, gt_i, u_i, de, dmf_o, act_o, dg_o, du_o, got_g, got_u, *scratch):
@@ -564,16 +573,18 @@
     dm_pair = cube.pair(dm_i, dmf.at[mine_t])
 
     def in_copies(p):
-        return [pltpu.make_async_copy(src.at[p], fin.at[p % 2, i], isem.at[i, p]) for i, src in enumerate((gt_i, u_i))]
+        slot = lax.rem(p, 2)
+        return [pltpu.make_async_copy(src.at[p], fin.at[slot, i], isem.at[i, slot]) for i, src in enumerate((gt_i, u_i))]
 
     def out_copies(p):
-        return [pltpu.make_async_copy(fout.at[p % 2, i], dst.at[p], osem.at[i, p]) for i, dst in enumerate((act_o, dg_o, du_o))]
+        slot = lax.rem(p, 2)
+        return [pltpu.make_async_copy(fout.at[slot, i], dst.at[p], osem.at[i, slot]) for i, dst in enumerate((act_o, dg_o, du_o))]
 
     def send_copies(p):
-        dev = (cube.m, 1 - c)
+        slot = lax.rem(p, 2)
         return [
             pltpu.make_async_remote_copy(
-                src_ref=part.at[p % 2, i], dst_ref=dst.at[p], send_sem=gsend.at[i, p], recv_sem=grecv.at[i, p], device_id=dev, device_id_type=MESH
+                src_ref=part.at[slot, i], dst_ref=dst.at[p], send_sem=gsend.at[i, p], recv_sem=grecv.at[i, p], device_id=(cube.m, 1 - c), device_id_type=MESH
             )
             for i, dst in enumerate((got_g, got_u))
         ]
@@ -589,19 +600,24 @@
     step = cube.ag_start(gb, ag_sems)
     dm_pair.start()
     cube.finish([dm_copy, wd_copy, a_copy])
-    tile = min(512, t)
-    tiles = t // tile
-    for p in range(PARTS):
-        if p + 1 < PARTS:
+
+    def chunk_work(p, first=False):
+        @pl.when(p + 1 < PARTS)
+        def _():
             cube.start(in_copies(p + 1))
+
         cube.finish(in_copies(p))
-        if p >= 2:
+
+        @pl.when(p >= 2)
+        def _():
             drain(p - 2)
-        src, dst, res = fin.at[p % 2], fout.at[p % 2], part.at[p % 2]
-
-        def body(half, i):
-            at = span(half * tiles + i, tile)
-            d_act = nt(dmf[at, :], wd[pl.ds(p * fc, fc), :])
+
+        slot = lax.rem(p, 2)
+        src, dst, res = fin.at[slot], fout.at[slot], part.at[slot]
+
+        def body(half):
+            at = span(half, t)
+            d_act = nt(dmf[at, :], wd[span(p, fc), :])
             gate = src[0, at, :].astype(F32)
             up = src[1, at, :].astype(F32)
             sig = jax.nn.sigmoid(gate)
@@ -610,18 +626,26 @@
             for which, v in enumerate(outs):
                 dst[which, at, :] = v.astype(BF16)
 
-        if p == 0:
-            loop(0, tiles, functools.partial(body, c))
+        if first:
+            body(c)
             dm_pair.wait()
             dm_out.start()
-            loop(0, tiles, functools.partial(body, 1 - c))
+            body(1 - c)
         else:
-            loop(0, 2 * tiles, functools.partial(body, 0))
+            loop(0, 2, body)
         for which in range(2):
             res[which] = nn(aoth[...], dst[which + 1])
         cube.start(out_copies(p) + send_copies(p))
-        if step > 0 and p % 2 == 0:
+
+    chunk_work(0, True)
+    step = cube.ag_next(gb, ag_sems, step)
+    p = 1
+    while p < PARTS:
+        q = min(p + 2, PARTS)
+        loop(p, q, chunk_work)
+        if step >= 0:
             step = cube.ag_next(gb, ag_sems, step)
+        p = q
     while step >= 0:
         step = cube.ag_next(gb, ag_sems, step)
     cube.collect(gb, nat)
@@ -653,18 +677,25 @@
 
 
 def weight_kernel(loss, de, at_i, dg, du, act, dmf_i, got_g, got_u, loss_o, de_o, og, ou, od, *scratch):
-    aown, dmf, ring, gring, ostage, dstage, de_s, de_t, lsem, rsem, gsem, osem, xsem = scratch
+    aown, dmf, ring, abuf, gring, ostage, dstage, de_s, de_t, lsem, rsem, asem, gsem, osem, dsem, xsem = scratch
     c = lax.axis_index("fsdp")
     depth, fc = ring.shape[0], ring.shape[-1]
     parts, half_f = dg.shape[0], dg.shape[0] * fc
+    quad = abuf.shape[-1] // fc
     local = Local(lsem)
     a_copy, dm_copy = local(at_i.at[span(c, aown.shape[0])], aown), local(dmf_i, dmf)
     de_in, de_out = local(de, de_s), local(de_t, de_o)
 
     def reads(p):
         slot = lax.rem(p, depth)
-        grads = [pltpu.make_async_copy(src.at[p], ring.at[slot, i], rsem.at[i, slot]) for i, src in enumerate((dg, du, act))]
-        return grads, [pltpu.make_async_copy(src.at[p], gring.at[slot, i], gsem.at[i, slot]) for i, src in enumerate((got_g, got_u))]
+        return [pltpu.make_async_copy(src.at[p], ring.at[slot, i], rsem.at[i, slot]) for i, src in enumerate((dg, du))]
+
+    def got(p):
+        slot = lax.rem(p, depth)
+        return [pltpu.make_async_copy(src.at[p], gring.at[slot, i], gsem.at[i, slot]) for i, src in enumerate((got_g, got_u))]
+
+    def acts(q):
+        return [pltpu.make_async_copy(act.at[q * quad + i], abuf.at[q, :, pl.ds(i * fc, fc)], asem.at[q, i]) for i in range(quad)]
 
     def columns(half, p):
         return pl.ds(pl.multiple_of(half * half_f + p * fc, fc), fc)
@@ -675,21 +706,24 @@
 
     def writes(p):
         slot = lax.rem(p, 2)
-        out = [pltpu.make_async_copy(ostage.at[slot, i], dst.at[:, columns(c, p)], osem.at[i, slot]) for i, dst in enumerate((og, ou))]
-        return out + [pltpu.make_async_copy(dstage.at[slot], od.at[span(p, fc)], osem.at[2, slot])]
+        return [pltpu.make_async_copy(ostage.at[slot, i], dst.at[:, columns(c, p)], osem.at[i, slot]) for i, dst in enumerate((og, ou))]
+
+    def down(q):
+        return pltpu.make_async_copy(dstage.at[q], od.at[span(q, quad * fc)], dsem.at[q])
 
     def each(copies, verb):
         for copy in copies:
             getattr(copy, verb)()
 
     def fetch(p):
-        grads, got = reads(p)
-        each(grads + got, "start")
+        each(reads(p) + got(p), "start")
 
     a_copy.start()
     fetch(0)
+    fetch(1)
+    each(acts(0), "start")
     dm_copy.start()
-    for p in range(1, depth):
+    for p in range(2, depth):
         fetch(p)
     de_in.start()
     a_copy.wait()
@@ -697,10 +731,9 @@
 
     def body(p):
         slot, oslot = lax.rem(p, depth), lax.rem(p, 2)
-        grads, got = reads(p)
-        each(got, "wait")
+        each(got(p), "wait")
         each(passes(p), "start")
-        each(grads, "wait")
+        each(reads(p), "wait")
 
         @pl.when(p >= 2)
         def _():
@@ -708,12 +741,6 @@
 
         for i in range(2):
             ostage[oslot, i] = nn(aown[...], ring[slot, i])
-
-        @pl.when(p == 0)
-        def _():
-            dm_copy.wait()
-
-        dstage[oslot] = tn(ring[slot, 2], dmf[...])
         each(writes(p), "start")
 
         @pl.when(p >= 1)
@@ -724,11 +751,24 @@
         def _():
             fetch(p - 1 + depth)
 
-    loop(0, parts, body)
+    def group(q):
+        loop(q * quad, (q + 1) * quad, body)
+
+        @pl.when(q == 0)
+        def _():
+            each(acts(1), "start")
+            dm_copy.wait()
+
+        each(acts(q), "wait")
+        dstage[q] = tn(abuf[q], dmf[...])
+        down(q).start()
+
+    loop(0, parts // quad, group)
     de_in.wait()
     de_t[...] = de_s[pl.ds(0, de_t.shape[0]), :]
     de_out.start()
     each(passes(parts - 1) + writes(parts - 2) + writes(parts - 1), "wait")
+    each([down(q) for q in range(parts // quad)], "wait")
     de_out.wait()
 
 
@@ -857,16 +897,19 @@
             scratch_shapes=[
                 pltpu.VMEM((half_d, 2 * t), BF16),
                 pltpu.VMEM((2 * t, d), BF16),
-                pltpu.VMEM((depth, 3, 2 * t, fc), BF16),
+                pltpu.VMEM((depth, 2, 2 * t, fc), BF16),
+                pltpu.VMEM((2, 2 * t, half_f // 2), BF16),
                 pltpu.VMEM((depth, 2, half_d, fc), F32),
                 pltpu.VMEM((2, 2, half_d, fc), F32),
-                pltpu.VMEM((2, fc, d), F32),
+                pltpu.VMEM((2, half_f // 2, d), F32),
                 pltpu.VMEM((vb, d), F32),
                 pltpu.VMEM((real, d), F32),
                 dma((4,)),
-                dma((3, depth)),
                 dma((2, depth)),
-                dma((3, 2)),
+                dma((2, PARTS // 2)),
+                dma((2, depth)),
+                dma((2, 2)),
+                dma((2,)),
                 dma((2, depth)),
             ],
             compiler_params=pltpu.CompilerParams(vmem_limit_bytes=VMEM_LIMIT, has_side_effects=True),

time: 214 us -> 213 us (level)
    pallas_call x1, Pallas kernels: 82.7 us -> 78.6 us  [device_step(): pl.pallas_call(functools.partial(head_kernel, cube, vb, real, num_tokens)...]
where the time goes in v4:
time: 213 us
  Pallas kernels  212 us (100%)
    pallas_call x1, Pallas kernels, device_step(): pl.pallas_call(functools.partial(head_kernel, cube, vb, real, num_tokens)...  78.6 us
    pallas_call x1, Pallas kernels, device_step(): pl.pallas_call(functools.partial(embed_kernel, cube, vb), out_shape=(sds(...  54.2 us
    pallas_call x1, Pallas kernels, device_step(): pl.pallas_call(functools.partial(table_kernel, cube, vb, real), out_shape...  48.3 us
    pallas_call x1, Pallas kernels, device_step(): pl.pallas_call(weight_kernel, out_shape=(sds((1, 1), F32), sds((real, d),...  30.8 us

profile of v4, /device:TPU:1, one launch (start us, length us, event | category | flops | bytes accessed | tf_op | source)
XLA Modules:
  0.0 212.7 jit_solution(9509468194061981006)
XLA Ops:
  0.6 54.2 %embed.1 = (bf16[1024,1024]{1,0:T(8,128)(2,1)}, bf16[800,1024]{1,0:T(8,128)(2,1)}, bf16[1024,2048]{1,0:T(8,128)(2,1)}, bf16[1024,2048]{1,0:T(8,128)(2,1)}, f32[1...) custom-call(s32[1,1024]{1,0:T(1,128)} %ids.3, ...), custom_call_target="tpu_custom_call" | custom-call | tf_op jit(solution)/shard_map/embed/pallas_call | solution.py:803
  54.8 78.6 %head.1 = (bf16[1024,1024]{1,0:T(8,128)(2,1)}, f32[1,1]{1,0:T(1,128)}, f32[800,1024]{1,0:T(8,128)}, f32[16,1024]{1,0:T(8,128)}, bf16[1024,2048]{1,0:T(8,128)(2,1...) custom-call(bf16[1024,1024]{1,0:T(8,128)(2,1)} %get-tuple-element.32.hn_i, ...), custom_call_target="tpu_custom_call" | custom-call | tf_op jit(solution)/shard_map/head/pallas_call | solution.py:828
  133.4 48.3 %table.1 = (f32[400,1024]{1,0:T(8,128)}, bf16[2048,1024]{1,0:T(8,128)(2,1)}, bf16[8,2048,256]{2,1,0:T(8,128)(2,1)}, bf16[8,2048,256]{2,1,0:T(8,128)(2,1)}, bf16[...) custom-call(s32[1,1024]{1,0:T(1,128)} %ids.3, f32[16,1024]{1,0:T(8,128)} %get-tuple-element.41.dx_own, ...), custom_call_target="tpu_custom_call" | custom-call | tf_op jit(solution)/shard_map/table/pallas_call | solution.py:863
  181.7 30.8 %weights.1 = (f32[1,1]{1,0:T(1,128)}, f32[393,1024]{1,0:T(8,128)}, f32[512,4096]{1,0:T(8,128)}, f32[512,4096]{1,0:T(8,128)}, f32[2048,1024]{1,0:T(8,128)}) custom-call(f32[1,1]{1,0:T(1,128)} %get-tuple-element.40.loss, f32[400,1024]{1,0:T(8,128)} %get-tuple-element.47.de, bf16[1024,2048]{1,0:T(8,128)(2,1)} %get-tuple-element.44.at_i, ...), custom_call_target="tpu_custom_call" | custom-call | tf_op jit(solution)/shard_map/weights/pallas_call | solution.py:892

commit v5 on v4

--- a/solution.py
+++ b/solution.py
@@ -640,33 +640,31 @@
     chunk_work(0, True)
     step = cube.ag_next(gb, ag_sems, step)
     p = 1
-    while p < PARTS:
-        q = min(p + 2, PARTS)
-        loop(p, q, chunk_work)
+    while p + 1 < PARTS:
+        loop(p, p + 2, chunk_work)
         if step >= 0:
             step = cube.ag_next(gb, ag_sems, step)
-        p = q
+        p += 2
     while step >= 0:
         step = cube.ag_next(gb, ag_sems, step)
     cube.collect(gb, nat)
     cube.finish([deh_copy, dm_out])
     chunk = min(256, t)
 
-    def scatter(half, i):
+    def scatter(i):
         at = span(i, chunk)
-        rows = pl.ds(half * vb, vb)
-        hot = one_hot(vb, table_rows(cube, real, vb, ids[:, at]) - half * vb)
+        hot = one_hot(2 * vb, table_rows(cube, real, vb, ids[:, at]))
         val = nat[at, :]
         hi = val.astype(BF16)
         rest = val - hi.astype(F32)
         mid = rest.astype(BF16)
         low = (rest - mid.astype(F32)).astype(BF16)
-        mix[rows, :] = mix[rows, :] + ((nn(hot, low) + nn(hot, mid)) + nn(hot, hi))
-
-    loop(0, t // chunk, functools.partial(scatter, 1))
+        mix[...] = mix[...] + ((nn(hot, low) + nn(hot, mid)) + nn(hot, hi))
+
+    loop(0, t // chunk, scatter)
     e_pair = cube.pair(mix.at[pl.ds(vb, vb)], de_r)
     e_pair.start()
-    loop(0, t // chunk, functools.partial(scatter, 0))
+    loop(PARTS - 1, PARTS, chunk_work)
     drain(PARTS - 2)
     drain(PARTS - 1)
     for p in range(PARTS):
@@ -677,25 +675,18 @@
 
 
 def weight_kernel(loss, de, at_i, dg, du, act, dmf_i, got_g, got_u, loss_o, de_o, og, ou, od, *scratch):
-    aown, dmf, ring, abuf, gring, ostage, dstage, de_s, de_t, lsem, rsem, asem, gsem, osem, dsem, xsem = scratch
+    aown, dmf, ring, gring, ostage, dstage, de_s, de_t, lsem, rsem, gsem, osem, xsem = scratch
     c = lax.axis_index("fsdp")
     depth, fc = ring.shape[0], ring.shape[-1]
     parts, half_f = dg.shape[0], dg.shape[0] * fc
-    quad = abuf.shape[-1] // fc
     local = Local(lsem)
     a_copy, dm_copy = local(at_i.at[span(c, aown.shape[0])], aown), local(dmf_i, dmf)
     de_in, de_out = local(de, de_s), local(de_t, de_o)
 
     def reads(p):
         slot = lax.rem(p, depth)
-        return [pltpu.make_async_copy(src.at[p], ring.at[slot, i], rsem.at[i, slot]) for i, src in enumerate((dg, du))]
-
-    def got(p):
-        slot = lax.rem(p, depth)
-        return [pltpu.make_async_copy(src.at[p], gring.at[slot, i], gsem.at[i, slot]) for i, src in enumerate((got_g, got_u))]
-
-    def acts(q):
-        return [pltpu.make_async_copy(act.at[q * quad + i], abuf.at[q, :, pl.ds(i * fc, fc)], asem.at[q, i]) for i in range(quad)]
+        grads = [pltpu.make_async_copy(src.at[p], ring.at[slot, i], rsem.at[i, slot]) for i, src in enumerate((dg, du, act))]
+        return grads, [pltpu.make_async_copy(src.at[p], gring.at[slot, i], gsem.at[i, slot]) for i, src in enumerate((got_g, got_u))]
 
     def columns(half, p):
         return pl.ds(pl.multiple_of(half * half_f + p * fc, fc), fc)
@@ -706,34 +697,36 @@
 
     def writes(p):
         slot = lax.rem(p, 2)
-        return [pltpu.make_async_copy(ostage.at[slot, i], dst.at[:, columns(c, p)], osem.at[i, slot]) for i, dst in enumerate((og, ou))]
-
-    def down(q):
-        return pltpu.make_async_copy(dstage.at[q], od.at[span(q, quad * fc)], dsem.at[q])
+        out = [pltpu.make_async_copy(ostage.at[slot, i], dst.at[:, columns(c, p)], osem.at[i, slot]) for i, dst in enumerate((og, ou))]
+        return out + [pltpu.make_async_copy(dstage.at[slot], od.at[span(p, fc)], osem.at[2, slot])]
 
     def each(copies, verb):
         for copy in copies:
             getattr(copy, verb)()
 
     def fetch(p):
-        each(reads(p) + got(p), "start")
+        grads, got = reads(p)
+        each(grads + got, "start")
 
     a_copy.start()
     fetch(0)
+    a_copy.wait()
+    dm_copy.start()
     fetch(1)
-    each(acts(0), "start")
-    dm_copy.start()
-    for p in range(2, depth):
-        fetch(p)
-    de_in.start()
-    a_copy.wait()
     loss_o[0, 0] = loss[0, 0]
 
     def body(p):
         slot, oslot = lax.rem(p, depth), lax.rem(p, 2)
-        each(got(p), "wait")
+        grads, got = reads(p)
+        each(grads, "wait")
+        each(got, "wait")
         each(passes(p), "start")
-        each(reads(p), "wait")
+
+        @pl.when(p == 0)
+        def _():
+            for later in range(2, depth):
+                fetch(later)
+            de_in.start()
 
         @pl.when(p >= 2)
         def _():
@@ -741,6 +734,12 @@
 
         for i in range(2):
             ostage[oslot, i] = nn(aown[...], ring[slot, i])
+
+        @pl.when(p == 0)
+        def _():
+            dm_copy.wait()
+
+        dstage[oslot] = tn(ring[slot, 2], dmf[...])
         each(writes(p), "start")
 
         @pl.when(p >= 1)
@@ -751,24 +750,11 @@
         def _():
             fetch(p - 1 + depth)
 
-    def group(q):
-        loop(q * quad, (q + 1) * quad, body)
-
-        @pl.when(q == 0)
-        def _():
-            each(acts(1), "start")
-            dm_copy.wait()
-
-        each(acts(q), "wait")
-        dstage[q] = tn(abuf[q], dmf[...])
-        down(q).start()
-
-    loop(0, parts // quad, group)
+    loop(0, parts, body)
     de_in.wait()
     de_t[...] = de_s[pl.ds(0, de_t.shape[0]), :]
     de_out.start()
     each(passes(parts - 1) + writes(parts - 2) + writes(parts - 1), "wait")
-    each([down(q) for q in range(parts // quad)], "wait")
     de_out.wait()
 
 
@@ -897,19 +883,16 @@
             scratch_shapes=[
                 pltpu.VMEM((half_d, 2 * t), BF16),
                 pltpu.VMEM((2 * t, d), BF16),
-                pltpu.VMEM((depth, 2, 2 * t, fc), BF16),
-                pltpu.VMEM((2, 2 * t, half_f // 2), BF16),
+                pltpu.VMEM((depth, 3, 2 * t, fc), BF16),
                 pltpu.VMEM((depth, 2, half_d, fc), F32),
                 pltpu.VMEM((2, 2, half_d, fc), F32),
-                pltpu.VMEM((2, half_f // 2, d), F32),
+                pltpu.VMEM((2, fc, d), F32),
                 pltpu.VMEM((vb, d), F32),
                 pltpu.VMEM((real, d), F32),
                 dma((4,)),
+                dma((3, depth)),
                 dma((2, depth)),
-                dma((2, PARTS // 2)),
-                dma((2, depth)),
-                dma((2, 2)),
-                dma((2,)),
+                dma((3, 2)),
                 dma((2, depth)),
             ],
             compiler_params=pltpu.CompilerParams(vmem_limit_bytes=VMEM_LIMIT, has_side_effects=True),

time: 213 us -> 212 us (level)
    pallas_call x1, Pallas kernels: 30.8 us -> 28.4 us  [device_step(): pl.pallas_call(weight_kernel, out_shape=(sds((1, 1), F32), sds((real, d),...]
where the time goes in v5:
time: 212 us
  Pallas kernels  211 us (100%)
    pallas_call x1, Pallas kernels, device_step(): pl.pallas_call(functools.partial(head_kernel, cube, vb, real, num_tokens)...  78.6 us
    pallas_call x1, Pallas kernels, device_step(): pl.pallas_call(functools.partial(embed_kernel, cube, vb), out_shape=(sds(...  54.2 us
    pallas_call x1, Pallas kernels, device_step(): pl.pallas_call(functools.partial(table_kernel, cube, vb, real), out_shape...  49.8 us
    pallas_call x1, Pallas kernels, device_step(): pl.pallas_call(weight_kernel, out_shape=(sds((1, 1), F32), sds((real, d),...  28.4 us

profile of v5, /device:TPU:1, one launch (start us, length us, event | category | flops | bytes accessed | tf_op | source)
XLA Modules:
  0.0 211.9 jit_solution(8065661869013799907)
XLA Ops:
  0.6 54.2 %embed.1 = (bf16[1024,1024]{1,0:T(8,128)(2,1)}, bf16[800,1024]{1,0:T(8,128)(2,1)}, bf16[1024,2048]{1,0:T(8,128)(2,1)}, bf16[1024,2048]{1,0:T(8,128)(2,1)}, f32[1...) custom-call(s32[1,1024]{1,0:T(1,128)} %ids.3, ...), custom_call_target="tpu_custom_call" | custom-call | tf_op jit(solution)/shard_map/embed/pallas_call | solution.py:789
  54.8 78.6 %head.1 = (bf16[1024,1024]{1,0:T(8,128)(2,1)}, f32[1,1]{1,0:T(1,128)}, f32[800,1024]{1,0:T(8,128)}, f32[16,1024]{1,0:T(8,128)}, bf16[1024,2048]{1,0:T(8,128)(2,1...) custom-call(bf16[1024,1024]{1,0:T(8,128)(2,1)} %get-tuple-element.32.hn_i, ...), custom_call_target="tpu_custom_call" | custom-call | tf_op jit(solution)/shard_map/head/pallas_call | solution.py:814
  133.4 49.8 %table.1 = (f32[400,1024]{1,0:T(8,128)}, bf16[2048,1024]{1,0:T(8,128)(2,1)}, bf16[8,2048,256]{2,1,0:T(8,128)(2,1)}, bf16[8,2048,256]{2,1,0:T(8,128)(2,1)}, bf16[...) custom-call(s32[1,1024]{1,0:T(1,128)} %ids.3, f32[16,1024]{1,0:T(8,128)} %get-tuple-element.41.dx_own, ...), custom_call_target="tpu_custom_call" | custom-call | tf_op jit(solution)/shard_map/table/pallas_call | solution.py:849
  183.3 28.4 %weights.1 = (f32[1,1]{1,0:T(1,128)}, f32[393,1024]{1,0:T(8,128)}, f32[512,4096]{1,0:T(8,128)}, f32[512,4096]{1,0:T(8,128)}, f32[2048,1024]{1,0:T(8,128)}) custom-call(f32[1,1]{1,0:T(1,128)} %get-tuple-element.40.loss, f32[400,1024]{1,0:T(8,128)} %get-tuple-element.47.de, bf16[1024,2048]{1,0:T(8,128)(2,1)} %get-tuple-element.44.at_i, ...), custom_call_target="tpu_custom_call" | custom-call | tf_op jit(solution)/shard_map/weights/pallas_call | solution.py:878

commit v6 on v5

--- a/solution.py
+++ b/solution.py
@@ -640,31 +640,33 @@
     chunk_work(0, True)
     step = cube.ag_next(gb, ag_sems, step)
     p = 1
-    while p + 1 < PARTS:
-        loop(p, p + 2, chunk_work)
+    while p < PARTS:
+        q = min(p + 2, PARTS)
+        loop(p, q, chunk_work)
         if step >= 0:
             step = cube.ag_next(gb, ag_sems, step)
-        p += 2
+        p = q
     while step >= 0:
         step = cube.ag_next(gb, ag_sems, step)
     cube.collect(gb, nat)
     cube.finish([deh_copy, dm_out])
     chunk = min(256, t)
 
-    def scatter(i):
+    def scatter(half, i):
         at = span(i, chunk)
-        hot = one_hot(2 * vb, table_rows(cube, real, vb, ids[:, at]))
+        rows = pl.ds(half * vb, vb)
+        hot = one_hot(vb, table_rows(cube, real, vb, ids[:, at]) - half * vb)
         val = nat[at, :]
         hi = val.astype(BF16)
         rest = val - hi.astype(F32)
         mid = rest.astype(BF16)
         low = (rest - mid.astype(F32)).astype(BF16)
-        mix[...] = mix[...] + ((nn(hot, low) + nn(hot, mid)) + nn(hot, hi))
-
-    loop(0, t // chunk, scatter)
+        mix[rows, :] = mix[rows, :] + ((nn(hot, low) + nn(hot, mid)) + nn(hot, hi))
+
+    loop(0, t // chunk, functools.partial(scatter, 1))
     e_pair = cube.pair(mix.at[pl.ds(vb, vb)], de_r)
     e_pair.start()
-    loop(PARTS - 1, PARTS, chunk_work)
+    loop(0, t // chunk, functools.partial(scatter, 0))
     drain(PARTS - 2)
     drain(PARTS - 1)
     for p in range(PARTS):

time: 212 us -> 211 us (level)
  no operation moved by 1% of the time
where the time goes in v6:
time: 211 us; the launch traced here: 210 us
  Pallas kernels  209 us (99%)
    pallas_call x1, Pallas kernels, device_step(): pl.pallas_call(functools.partial(head_kernel, cube, vb, real, num_tokens)...  78.6 us
    pallas_call x1, Pallas kernels, device_step(): pl.pallas_call(functools.partial(embed_kernel, cube, vb), out_shape=(sds(...  54.2 us
    pallas_call x1, Pallas kernels, device_step(): pl.pallas_call(functools.partial(table_kernel, cube, vb, real), out_shape...  48.3 us
    pallas_call x1, Pallas kernels, device_step(): pl.pallas_call(weight_kernel, out_shape=(sds((1, 1), F32), sds((real, d),...  28.4 us

profile of v6, /device:TPU:1, one launch (start us, length us, event | category | flops | bytes accessed | tf_op | source)
XLA Modules:
  0.0 210.3 jit_solution(3161104411353988043)
XLA Ops:
  0.6 54.2 %embed.1 = (bf16[1024,1024]{1,0:T(8,128)(2,1)}, bf16[800,1024]{1,0:T(8,128)(2,1)}, bf16[1024,2048]{1,0:T(8,128)(2,1)}, bf16[1024,2048]{1,0:T(8,128)(2,1)}, f32[1...) custom-call(s32[1,1024]{1,0:T(1,128)} %ids.3, ...), custom_call_target="tpu_custom_call" | custom-call | tf_op jit(solution)/shard_map/embed/pallas_call | solution.py:791
  54.8 78.6 %head.1 = (bf16[1024,1024]{1,0:T(8,128)(2,1)}, f32[1,1]{1,0:T(1,128)}, f32[800,1024]{1,0:T(8,128)}, f32[16,1024]{1,0:T(8,128)}, bf16[1024,2048]{1,0:T(8,128)(2,1...) custom-call(bf16[1024,1024]{1,0:T(8,128)(2,1)} %get-tuple-element.32.hn_i, ...), custom_call_target="tpu_custom_call" | custom-call | tf_op jit(solution)/shard_map/head/pallas_call | solution.py:816
  133.4 48.3 %table.1 = (f32[400,1024]{1,0:T(8,128)}, bf16[2048,1024]{1,0:T(8,128)(2,1)}, bf16[8,2048,256]{2,1,0:T(8,128)(2,1)}, bf16[8,2048,256]{2,1,0:T(8,128)(2,1)}, bf16[...) custom-call(s32[1,1024]{1,0:T(1,128)} %ids.3, f32[16,1024]{1,0:T(8,128)} %get-tuple-element.41.dx_own, ...), custom_call_target="tpu_custom_call" | custom-call | tf_op jit(solution)/shard_map/table/pallas_call | solution.py:851
  181.7 28.4 %weights.1 = (f32[1,1]{1,0:T(1,128)}, f32[393,1024]{1,0:T(8,128)}, f32[512,4096]{1,0:T(8,128)}, f32[512,4096]{1,0:T(8,128)}, f32[2048,1024]{1,0:T(8,128)}) custom-call(f32[1,1]{1,0:T(1,128)} %get-tuple-element.40.loss, f32[400,1024]{1,0:T(8,128)} %get-tuple-element.47.de, bf16[1024,2048]{1,0:T(8,128)(2,1)} %get-tuple-element.44.at_i, ...), custom_call_target="tpu_custom_call" | custom-call | tf_op jit(solution)/shard_map/weights/pallas_call | solution.py:880
